TPU v7x, 32 devices: a whole 2x2x4 slice. The times are simulated.
32 devices in a mesh: light: 4 (over y, x), screen: 8 (over z, core).
Axes of the slice: x: 2, y: 2, z: 4, core: 2. Of those that a mesh axis runs over, the one named last changes fastest.
Arguments:
- density: float32 [128, 256, 512], P('screen', None, 'light'), may hold values from 0 to 1.09375, as said below
- albedo: float32 [128, 256, 512], P('screen', None, 'light'), may hold values from 0.2 to 1
- light_in: float32 [128, 256], replicated, may hold values from 0.5 to 1.5
- occupancy: int32 [8, 16, 32], P('screen', None, 'light'), may hold values 0 or 1
- phase: int32 [256, 512], replicated, may hold values from 0 to 15
- fractions: float32 [3, 16], replicated, may hold values from 0 to 1
Outputs:
- image: float32 [256, 512], P('screen', 'light')
- transmittance: float32 [256, 512], P('screen', 'light')
- lit_bricks: float32 [128, 256, 512], P('light', 'screen')
Inputs may be any that keep to these rules, and one draw needn't show every extreme that they name: `density`: nonnegative extinction of each cell. `occupancy`: 1 where the brick of 16 cells on a side is occupied.
All inputs are finite; a program needn't handle non-finite values. No bound on the sum of `occupancy` on one device may be relied on, other than what follows from the above.
Results may differ from a plain program's by a relative error of at most 0.0003.
Values sent between devices are 32-bit elements; how exact they have to be, the bound alone decides.
No kernel may reach another device: no remote copies, remote signals or barrier semaphores. Data moves between devices by JAX's collectives and lax.ppermute only.
A program may use at most 192 MiB of HBM per device.

v0:
```python
import jax
import jax.numpy as jnp
from jax import lax
from jax.sharding import PartitionSpec as P

BRICK = 16


def passed_along(value, axis, by):
    peers = lax.axis_size(axis)
    pairs = [(i, i + by) for i in range(peers) if 0 <= i + by < peers]
    return lax.ppermute(value, axis, pairs)


def carried_in(part, axis, combine, identity):
    place = lax.axis_index(axis)
    gathered = lax.all_gather(part, axis)
    state = jnp.zeros_like(part) + jnp.asarray(identity, part.dtype)

    def one(step, state):
        return combine(state, lax.dynamic_index_in_dim(gathered, step, 0, False))

    return lax.fori_loop(0, place, one, state)


def prefix_last(values):
    length = values.shape[-1]
    block = 128
    count = length // block
    shaped = values.reshape(values.shape[:-1] + (count, block))
    rowsidx = lax.broadcasted_iota(jnp.int32, (block, block), 0)
    colsidx = lax.broadcasted_iota(jnp.int32, (block, block), 1)
    upper = (rowsidx < colsidx).astype(jnp.float32)
    within = jnp.matmul(shaped, upper, precision=lax.Precision.HIGHEST)
    totals = jnp.sum(shaped, axis=-1)
    carried = jnp.cumsum(totals, axis=-1) - totals
    return (within + carried[..., None]).reshape(values.shape)


def prefix_first(values):
    length = values.shape[0]
    count = length // length
    shaped = values.reshape(count, length, -1)
    rowsidx = lax.broadcasted_iota(jnp.int32, (length, length), 0)
    colsidx = lax.broadcasted_iota(jnp.int32, (length, length), 1)
    lower = (colsidx < rowsidx).astype(jnp.float32)
    within = jnp.einsum("ij,bjr->bir", lower, shaped, precision=lax.Precision.HIGHEST)
    totals = jnp.sum(shaped, axis=1)
    carried = jnp.cumsum(totals, axis=0) - totals
    return (within + carried[:, None]).reshape(values.shape)


def corner_fractions(rays, fractions):
    levels = lax.broadcasted_iota(jnp.int32, (fractions.shape[1], 1, 1), 0)
    onehot = (rays[None] == levels).astype(jnp.float32)
    return jnp.einsum("kp,prc->krc", fractions, onehot, precision=lax.Precision.HIGHEST)


def resample(field, tail, weights, deep, cols):
    first = field[:, 0:cols]
    second = field[:, 1 : cols + 1]
    edge_first = tail[:, 0:cols]
    edge_second = tail[:, 1 : cols + 1]
    first_next = jnp.concatenate([first[:, :, 1:], edge_first], axis=2)
    second_next = jnp.concatenate([second[:, :, 1:], edge_second], axis=2)
    depth_w = weights[0]
    column_w = weights[1]
    light_w = weights[2]
    near = first + column_w * (second - first)
    further = first_next + column_w * (second_next - first_next)
    mixed = near + light_w * (further - near)
    lower = mixed[0:deep]
    higher = mixed[1 : deep + 1]
    return lower + depth_w * (higher - lower)


def composite(extinct, shaded):
    screened = prefix_first(extinct)
    part = jnp.sum(jnp.exp(-screened) * (1.0 - jnp.exp(-extinct)) * shaded, axis=0)
    return (part, jnp.sum(extinct, axis=0))


def finish(parts, totals):
    before = jnp.cumsum(totals, axis=0) - totals
    picture = jnp.sum(jnp.exp(-before) * parts, axis=0)
    return (picture, jnp.exp(-jnp.sum(totals, axis=0)))


def march_slabs(masked, lit, phase, fractions):
    slab_b, width_a, slab_l = masked.shape
    light_idx = lax.axis_index("light")
    rims = passed_along((masked[:2], lit[:2]), "screen", -1)
    dens_ext = jnp.pad(jnp.concatenate([masked, rims[0]], axis=0), ((0, 0), (0, 2), (0, 0)))
    lit_ext = jnp.pad(jnp.concatenate([lit, rims[1]], axis=0), ((0, 0), (0, 2), (0, 0)))
    tails = passed_along((dens_ext[:, :, :1], lit_ext[:, :, :1]), "light", -1)
    rays = lax.dynamic_slice_in_dim(phase, light_idx * slab_l, slab_l, 1)
    weights = corner_fractions(rays, fractions)
    extinct = resample(dens_ext, tails[0], weights, slab_b, width_a)
    shaded = resample(lit_ext, tails[1], weights, slab_b, width_a)
    part, total = composite(extinct, shaded)
    parts, totals = (
        lax.all_to_all(part[None], "screen", split_axis=1, concat_axis=0, tiled=True),
        lax.all_to_all(total[None], "screen", split_axis=1, concat_axis=0, tiled=True),
    )
    return finish(parts, totals)


def local(density, albedo, light_in, occupancy, phase, fractions):
    slab_b, width_a, slab_l = density.shape
    bricks_b, bricks_a, bricks_l = occupancy.shape
    masked = (
        density.reshape(bricks_b, BRICK, bricks_a, BRICK, bricks_l, BRICK)
        * occupancy.astype(jnp.float32)[:, None, :, None, :, None]
    ).reshape(density.shape)
    screen_idx = lax.axis_index("screen")
    local_depth = prefix_last(masked)
    totals = jnp.sum(masked, axis=2)
    before = carried_in(totals, "light", jnp.add, jnp.zeros_like(totals))
    incoming = lax.dynamic_slice_in_dim(light_in, screen_idx * slab_b, slab_b, 0)
    lit = albedo * incoming[:, :, None] * jnp.exp(-(local_depth + before[:, :, None]))
    lit_cam = lax.all_to_all(lit, "screen", split_axis=1, concat_axis=0, tiled=True)
    lit_cam = lax.all_to_all(lit_cam, "light", split_axis=0, concat_axis=2, tiled=True)
    picture, passing = march_slabs(masked, lit, phase, fractions)
    return (picture, passing, lit_cam)


def solution(mesh):
    return jax.shard_map(
        local,
        mesh=mesh,
        in_specs=(
            P("screen", None, "light"),
            P("screen", None, "light"),
            P(),
            P("screen", None, "light"),
            P(),
            P(),
        ),
        out_specs=(P("screen", "light"), P("screen", "light"), P("light", "screen", None)),
        check_vma=False,
    )
```

profile of v0, /device:TPU:0, one launch (start us, length us, event | category | flops | bytes accessed | tf_op | source)
XLA Modules:
  0.0 195.5 jit_solution(17380704200879934052)
XLA Ops:
  1.9 2.2 %fusion.35 = (f32[16,256]{1,0:T(8,128)S(1)}, f32[16,256,128]{2,1,0:T(8,128)S(1)}) fusion(f32[16,256,128]{2,1,0:T(8,128)} %param.8, f32[256,128]{1,0:T(8,128)S(1)} %mul.121), kind=kLoop, calls=%fused_computation.62 | loop fusion | flops 1044480 | bytes 4341760 | tf_op jit(solution)/shard_map/reduce_sum | solution.py:35
  4.2 9.7 %all-gather = f32[64,256]{1,0:T(8,128)S(1)} all-gather(f32[16,256]{1,0:T(8,128)S(1)} %get-tuple-element.35), channel_id=2, replica_groups=mesh['light'=4,'screen'=8] {'light'}, dimensions={0}, use_global_device_ids=true | all-gather | bytes 81920 | tf_op jit(solution)/shard_map/all_gather | solution.py:17
  14.6 3.8 %exponential_multiply_fusion = f32[16,256,128]{2,1,0:T(8,128)S(1)} fusion(f32[16,256,128]{2,1,0:T(8,128)} %param.9, f32[16,256,128]{2,1,0:T(8,128)S(1)} %get-tuple-element.36, f32[16,256]{1,0:T(8,128)S(1)} %get-tuple-element.26, f32[16,256]{1,0:T(8,128)S(1)} %sub.66, f32[16,256]{1,0:T(8,128)S(1)} %constant_dynamic-slice_fusion), kind=kOutput, calls=%fused_computation.42 | convolution fusion | flops 807944192 | bytes 6340608 | tf_op jit(solution)/shard_map/dot_general | solution.py:34
  21.1 10.6 %reshape.82 = f32[1,16,16,16,8,16]{5,4,3,2,1,0:T(8,128)} reshape(f32[16,256,128]{2,1,0:T(8,128)} %param.8) | data formatting | bytes 4194304 | tf_op jit(solution)/shard_map/reshape | solution.py:112
  31.7 1.9 slice_multiply_fusion
  37.9 1.7 pad_maximum_fusion.1
  39.6 2.1 %pad_slice_fusion.2 = f32[18,256,127]{2,1,0:T(8,128)} fusion(f32[18,256,128]{2,1,0:T(8,128)S(1)} %pad_maximum_fusion.1), kind=kLoop, calls=%fused_computation.25 | loop fusion | bytes 4700160 | tf_op jit(solution)/shard_map/slice | solution.py:65
  41.7 1.6 pad_slice_fusion.3
  44.4 2.2 %pad_slice_fusion.4 = f32[18,256,127]{2,1,0:T(8,128)} fusion(f32[18,256,128]{2,1,0:T(8,128)S(1)} %pad_maximum_fusion), kind=kLoop, calls=%fused_computation.27 | loop fusion | bytes 4700160 | tf_op jit(solution)/shard_map/slice | solution.py:65
  46.6 1.6 pad_slice_fusion.5
  48.2 2.7 %copy.33 = f32[18,258,1]{1,2,0:T(1,128)S(1)} copy(f32[18,258,1]{2,1,0:T(8,128)} %pad_slice_fusion.3) | data formatting | bytes 37152 | tf_op jit(solution)/shard_map/slice | solution.py:95
  52.2 2.7 %copy.30 = f32[18,258,1]{1,2,0:T(1,128)S(1)} copy(f32[18,258,1]{2,1,0:T(8,128)} %pad_slice_fusion.5) | data formatting | bytes 37152 | tf_op jit(solution)/shard_map/slice | solution.py:95
  56.5 3.7 %fusion.3 = f32[18,256,127]{2,1,0:T(8,128)} fusion(f32[2,256,128]{2,1,0:T(8,128)S(1)} %collective-permute-done.2, f32[16,256,128]{2,1,0:T(8,128)} %copy-done.3), kind=kLoop, calls=%fused_computation.9 | loop fusion | flops 585216 | bytes 4700160 | tf_op jit(solution)/shard_map/concatenate | solution.py:94
  60.2 2.1 %fusion.4 = f32[18,256,127]{2,1,0:T(8,128)} fusion(f32[2,256,128]{2,1,0:T(8,128)S(1)} %collective-permute-done, f32[16,256,128]{2,1,0:T(8,128)S(1)} %copy-done.7), kind=kLoop, calls=%fused_computation.10 | loop fusion | flops 585216 | bytes 4700160 | tf_op jit(solution)/shard_map/concatenate | solution.py:93
  62.4 2.1 %copy.35 = f32[18,256,1]{2,1,0:T(8,128)} copy(f32[18,256,1]{1,2,0:T(1,128)S(1)} %get-tuple-element.44) | data formatting | bytes 36864 | tf_op jit(solution)/shard_map/slice | solution.py:63
  64.6 2.2 %copy.34 = f32[18,256,1]{2,1,0:T(8,128)} copy(f32[18,256,1]{1,2,0:T(1,128)S(1)} %get-tuple-element.45) | data formatting | bytes 36864 | tf_op jit(solution)/shard_map/slice | solution.py:62
  66.8 2.1 %copy.32 = f32[18,256,1]{2,1,0:T(8,128)} copy(f32[18,256,1]{1,2,0:T(1,128)S(1)} %get-tuple-element.46) | data formatting | bytes 36864 | tf_op jit(solution)/shard_map/slice | solution.py:63
  69.0 2.1 %copy.31 = f32[18,256,1]{2,1,0:T(8,128)} copy(f32[18,256,1]{1,2,0:T(1,128)S(1)} %get-tuple-element.47) | data formatting | bytes 36864 | tf_op jit(solution)/shard_map/slice | solution.py:62
  71.1 12.0 %fusion.14 = (f32[18,256,128]{2,1,0:T(8,128)}, f32[18,256,128]{2,1,0:T(8,128)S(1)}) fusion(f32[18,256,1]{2,1,0:T(8,128)} %copy.34, f32[18,256,127]{2,1,0:T(8,128)} %fusion.3, f32[18,256,1]{2,1,0:T(8,128)} %copy.35, f32[18,256,127]{2,1,0:T(8,128)} %pad_slice_fusion.2, f32[18,256,128]{2,1,0:T(8,128)S(1)} %pad_maximum_fusion.1, f32[256,128]{1,0:T(8,128)S(1)} %bitcast.74, ...), kind=kLoop, calls=%fused_computation.24 | loop fusion | flops 12976128 | bytes 19136512 | tf_op jit(solution)/shard_map/add | solution.py:71
  83.2 2.3 %fusion.36 = (f32[256,128]{1,0:T(8,128)}, f32[16,256,128]{2,1,0:T(8,128)}) fusion(f32[18,256,128]{2,1,0:T(8,128)S(1)} %get-tuple-element.43, f32[256,128]{1,0:T(8,128)S(1)} %bitcast.72), kind=kLoop, calls=%fused_computation.63 | loop fusion | flops 2064384 | bytes 6553600 | tf_op jit(solution)/shard_map/reduce_sum | solution.py:80
  85.5 6.7 %all-to-all-start = ((f32[1,256,128]{2,0,1:T(1,128)}), f32[1,256,128]{2,0,1:T(1,128)S(1)}, u32[]{:S(2)}, u32[]{:S(2)}) async-start(f32[1,256,128]{2,0,1:T(1,128)} %bitcast.7), calls=%async_computation | async-start | bytes 262144 | tf_op jit(solution)/shard_map/all_to_all | solution.py:103
  92.2 2.5 %copy.36 = f32[16,256,128]{2,0,1:T(8,128)} copy(f32[16,256,128]{2,1,0:T(8,128)S(1)} %copy-done.4) | data formatting | bytes 4194304 | tf_op jit(solution)/shard_map/mul | solution.py:120
  94.7 4.2 %all-to-all-done = f32[1,256,128]{2,0,1:T(1,128)S(1)} async-done(((f32[1,256,128]{2,0,1:T(1,128)}), f32[1,256,128]{2,0,1:T(1,128)S(1)}, u32[]{:S(2)}, u32[]{:S(2)}) %all-to-all-start) | async-done | bytes 131104 | tf_op jit(solution)/shard_map/all_to_all | solution.py:103
  98.9 4.4 %all-to-all-start.2 = ((f32[16,256,128]{2,0,1:T(8,128)}), f32[16,256,128]{2,0,1:T(8,128)}, u32[]{:S(2)}, u32[]{:S(2)}) async-start(f32[16,256,128]{2,0,1:T(8,128)} %copy.36), calls=%async_computation.2 | async-start | bytes 4194304 | tf_op jit(solution)/shard_map/all_to_all | solution.py:121
  104.2 2.5 %fusion.24 = f32[2,8,256,128]{3,1,2,0:T(8,128)S(1)} fusion(f32[2,8,256,128]{3,2,1,0:T(8,128)S(1)} %bitcast.67, f32[32768]{0:T(1024)S(1)} %subtract_bitcast_fusion), kind=kOutput, calls=%fused_computation.45 | convolution fusion | flops 101712128 | bytes 4325376 | tf_op jit(solution)/shard_map/ij,bjr->bir/dot_general | solution.py:47
  109.7 42.7 %all-to-all-done.2 = f32[16,256,128]{2,0,1:T(8,128)} async-done(((f32[16,256,128]{2,0,1:T(8,128)}), f32[16,256,128]{2,0,1:T(8,128)}, u32[]{:S(2)}, u32[]{:S(2)}) %all-to-all-start.2) | async-done | bytes 2097184 | tf_op jit(solution)/shard_map/all_to_all | solution.py:121
  152.3 3.4 %all-to-all-start.1 = ((f32[1,256,128]{2,0,1:T(1,128)}), f32[1,256,128]{2,0,1:T(1,128)S(1)}, u32[]{:S(2)}, u32[]{:S(2)}) async-start(f32[1,256,128]{2,0,1:T(1,128)} %bitcast.14), calls=%async_computation.1 | async-start | bytes 262144 | tf_op jit(solution)/shard_map/all_to_all | solution.py:102
  155.7 3.5 %copy.38 = f32[8,16,32,128]{3,2,1,0:T(8,128)} copy(f32[8,16,32,128]{3,1,2,0:T(8,128)} %bitcast.18) | data formatting | bytes 4194304 | tf_op jit(solution)/shard_map/all_to_all | solution.py:121
  159.3 3.1 %all-to-all-done.1 = f32[1,256,128]{2,0,1:T(1,128)S(1)} async-done(((f32[1,256,128]{2,0,1:T(1,128)}), f32[1,256,128]{2,0,1:T(1,128)S(1)}, u32[]{:S(2)}, u32[]{:S(2)}) %all-to-all-start.1) | async-done | bytes 131104 | tf_op jit(solution)/shard_map/all_to_all | solution.py:102
  162.4 6.9 %all-to-all-start.3 = ((f32[128,32,128]{2,1,0:T(8,128)}), f32[128,32,128]{2,1,0:T(8,128)S(1)}, u32[]{:S(2)}, u32[]{:S(2)}) async-start(f32[128,32,128]{2,1,0:T(8,128)} %bitcast.19), calls=%async_computation.3 | async-start | bytes 4194304 | tf_op jit(solution)/shard_map/all_to_all | solution.py:122
  170.6 23.3 %all-to-all-done.3 = f32[128,32,128]{2,1,0:T(8,128)S(1)} async-done(((f32[128,32,128]{2,1,0:T(8,128)}), f32[128,32,128]{2,1,0:T(8,128)S(1)}, u32[]{:S(2)}, u32[]{:S(2)}) %all-to-all-start.3) | async-done | bytes 2097184 | tf_op jit(solution)/shard_map/all_to_all | solution.py:122
  193.9 1.6 copy.51
  (56 shorter events, 18.2 us)
Async XLA Ops:
  0.6 35.5 %copy-start = (s32[256,512]{1,0:T(8,128)S(1)}, s32[256,512]{1,0:T(8,128)}, u32[]{:S(2)}) copy-start(s32[256,512]{1,0:T(8,128)} %param.12) | copy-start | bytes 1572868
  4.1 14.3 %copy-start.5 = (f32[16,256,128]{2,1,0:T(8,128)}, f32[16,256,128]{2,1,0:T(8,128)S(1)}, u32[]{:S(2)}) copy-start(f32[16,256,128]{2,1,0:T(8,128)S(1)} %get-tuple-element.36) | copy-start | bytes 6291460
  18.5 1.3 copy-start.3
  19.8 18.1 %collective-permute-start.2 = (f32[2,256,128]{2,1,0:T(8,128)S(1)}, f32[2,256,128]{2,1,0:T(8,128)S(1)}, u32[]{:S(2)}, u32[]{:S(2)}) collective-permute-start(f32[2,256,128]{2,1,0:T(8,128)S(1)} %slice.105), channel_id=1, source_target_pairs={{1,0},{2,1},{3,2},{4,3},{5,4},{6,5},{7,6},{9,8},{10,9},{11,10},{12... | collective-permute-start | bytes 786440 | tf_op jit(solution)/shard_map/ppermute | solution.py:12
  33.6 2.6 %copy-start.12 = (f32[3,16]{1,0:T(4,128)S(1)}, f32[3,16]{1,0:T(4,128)}, u32[]{:S(2)}) copy-start(f32[3,16]{1,0:T(4,128)} %param.13) | copy-start | bytes 580
  34.8 8.5 %collective-permute-start = (f32[2,256,128]{2,1,0:T(8,128)}, f32[2,256,128]{2,1,0:T(8,128)S(1)}, u32[]{:S(2)}, u32[]{:S(2)}) collective-permute-start(f32[2,256,128]{2,1,0:T(8,128)} %slice.74), channel_id=1, source_target_pairs={{1,0},{2,1},{3,2},{4,3},{5,4},{6,5},{7,6},{9,8},{10,9},{11,10},{12... | collective-permute-start | bytes 786440 | tf_op jit(solution)/shard_map/ppermute | solution.py:12
  41.7 2.5 %copy-start.6 = (f32[16,256,128]{2,1,0:T(8,128)S(1)}, f32[16,256,128]{2,1,0:T(8,128)}, u32[]{:S(2)}) copy-start(f32[16,256,128]{2,1,0:T(8,128)} %copy-done.5) | copy-start | bytes 6291460
  44.4 2.2 %copy-start.2 = (f32[18,256,128]{2,1,0:T(8,128)}, f32[18,256,128]{2,1,0:T(8,128)S(1)}, u32[]{:S(2)}) copy-start(f32[18,256,128]{2,1,0:T(8,128)S(1)} %pad_maximum_fusion) | copy-start | bytes 7077892
  50.9 11.4 %collective-permute-start.3 = (f32[18,258,1]{1,2,0:T(1,128)S(1)}, f32[18,258,1]{1,2,0:T(1,128)S(1)}, u32[]{:S(2)}, u32[]{:S(2)}) collective-permute-start(f32[18,258,1]{1,2,0:T(1,128)S(1)} %copy.33), channel_id=1, source_target_pairs={{8,0},{16,8},{24,16},{9,1},{17,9},{25,17},{10,2},{18,10},{26,18},{... | collective-permute-start | bytes 55736 | tf_op jit(solution)/shard_map/ppermute | solution.py:12
  54.9 5.3 %copy-start.7 = (f32[16,256,128]{2,1,0:T(8,128)S(1)}, f32[16,256,128]{2,1,0:T(8,128)}, u32[]{:S(2)}) copy-start(f32[16,256,128]{2,1,0:T(8,128)} %copy-done.5) | copy-start | bytes 6291460
  54.9 11.8 %collective-permute-start.1 = (f32[18,258,1]{1,2,0:T(1,128)S(1)}, f32[18,258,1]{1,2,0:T(1,128)S(1)}, u32[]{:S(2)}, u32[]{:S(2)}) collective-permute-start(f32[18,258,1]{1,2,0:T(1,128)S(1)} %copy.30), channel_id=1, source_target_pairs={{8,0},{16,8},{24,16},{9,1},{17,9},{25,17},{10,2},{18,10},{26,18},{... | collective-permute-start | bytes 55736 | tf_op jit(solution)/shard_map/ppermute | solution.py:12
  66.8 4.3 %copy-start.10 = (f32[1,256,128]{2,0,1:T(1,128)S(1)}, f32[1,256,128]{2,0,1:T(1,128)}, u32[]{:S(2)}) copy-start(f32[1,256,128]{2,0,1:T(1,128)} %get-tuple-element.40) | copy-start | bytes 393220
  66.8 4.3 %copy-start.11 = (f32[1,256,128]{2,0,1:T(1,128)S(1)}, f32[1,256,128]{2,0,1:T(1,128)}, u32[]{:S(2)}) copy-start(f32[1,256,128]{2,0,1:T(1,128)} %get-tuple-element.41) | copy-start | bytes 393220
  83.2 9.0 %copy-start.4 = (f32[16,256,128]{2,1,0:T(8,128)S(1)}, f32[16,256,128]{2,1,0:T(8,128)}, u32[]{:S(2)}) copy-start(f32[16,256,128]{2,1,0:T(8,128)} %copy-done.3) | copy-start | bytes 6291460
  85.5 13.4 %all-to-all-start = ((f32[1,256,128]{2,0,1:T(1,128)}), f32[1,256,128]{2,0,1:T(1,128)S(1)}, u32[]{:S(2)}, u32[]{:S(2)}) async-start(f32[1,256,128]{2,0,1:T(1,128)} %bitcast.7), calls=%async_computation | async-start | bytes 262144 | tf_op jit(solution)/shard_map/all_to_all | solution.py:103
  94.7 9.5 %copy-start.8 = (f32[16,256,128]{2,1,0:T(8,128)S(1)}, f32[16,256,128]{2,1,0:T(8,128)}, u32[]{:S(2)}) copy-start(f32[16,256,128]{2,1,0:T(8,128)} %get-tuple-element.38) | copy-start | bytes 6291460
  98.9 53.4 %all-to-all-start.2 = ((f32[16,256,128]{2,0,1:T(8,128)}), f32[16,256,128]{2,0,1:T(8,128)}, u32[]{:S(2)}, u32[]{:S(2)}) async-start(f32[16,256,128]{2,0,1:T(8,128)} %copy.36), calls=%async_computation.2 | async-start | bytes 4194304 | tf_op jit(solution)/shard_map/all_to_all | solution.py:121
  106.7 1.7 copy-start.9
  152.3 10.1 %all-to-all-start.1 = ((f32[1,256,128]{2,0,1:T(1,128)}), f32[1,256,128]{2,0,1:T(1,128)S(1)}, u32[]{:S(2)}, u32[]{:S(2)}) async-start(f32[1,256,128]{2,0,1:T(1,128)} %bitcast.14), calls=%async_computation.1 | async-start | bytes 262144 | tf_op jit(solution)/shard_map/all_to_all | solution.py:102
  162.4 31.5 %all-to-all-start.3 = ((f32[128,32,128]{2,1,0:T(8,128)}), f32[128,32,128]{2,1,0:T(8,128)S(1)}, u32[]{:S(2)}, u32[]{:S(2)}) async-start(f32[128,32,128]{2,1,0:T(8,128)} %bitcast.19), calls=%async_computation.3 | async-start | bytes 4194304 | tf_op jit(solution)/shard_map/all_to_all | solution.py:122
  169.4 26.2 %copy-start.1 = (s32[256,512]{1,0:T(8,128)S(1)}, s32[256,512]{1,0:T(8,128)}, u32[]{:S(2)}) copy-start(s32[256,512]{1,0:T(8,128)} %param.12) | copy-start | bytes 1572868
where the time goes:
time: 197 us; the launch traced here: 196 us
  waiting for transfers between devices  73.3 us (37%)
  local copies, waits for them, and re-layouts  47.3 us (24%)
  other arithmetic  30.4 us (15%)
  starting transfers between devices  26.8 us (14%)
  blocking collectives  9.72 us (5%)
  matrix products  7 us (4%)
    all_to_all x1, waiting for transfers between devices, local(): lax.all_to_all(lit, 'screen', split_axis=1, concat_axis=0, tiled=True)  42.7 us
    all_to_all x1, waiting for transfers between devices, local(): lax.all_to_all(lit_cam, 'light', split_axis=0, concat_axis=2, tiled=True)  23.3 us
    add x1, other arithmetic, resample(): mixed = near + light_w * (further - near)  12 us
    reshape x1, local copies, waits for them, and re-layouts, local(): density.reshape(bricks_b, BRICK, bricks_a, BRICK, bricks_l, BRICK)  10.6 us
    all_gather x1, blocking collectives, carried_in(): gathered = lax.all_gather(part, axis)  9.72 us
    slice x4, local copies, waits for them, and re-layouts, march_slabs(): tails = passed_along((dens_ext[:, :, :1], lit_ext[:, :, :1]), 'light', -1)  8.64 us
    all_to_all x1, starting transfers between devices, local(): lax.all_to_all(lit_cam, 'light', split_axis=0, concat_axis=2, tiled=True)  6.94 us
    all_to_all x1, starting transfers between devices, march_slabs(): lax.all_to_all(total[None], 'screen', split_axis=1, concat_axis=0, tiled=...  6.67 us
  transfers between devices with their start and end apart: 8, of which 4 were waited for; matrix products, arithmetic and copies ran while one was open for 24% of the time, Pallas kernels for 0%

commit v1 on v0

v1 whole, which is shorter than its diff:
```python
import functools

import jax
import jax.numpy as jnp
from jax import lax
from jax.experimental import pallas as pl
from jax.experimental.pallas import tpu as pltpu
from jax.sharding import PartitionSpec as P


BRICK = 16
SUB = 8


def bit_reversed(value, size):
    out = 0
    bit = 1
    while bit < size:
        out = out * 2 + ((value // bit) & 1 if isinstance(value, int) else lax.div(value, bit) & 1)
        bit *= 2
    return out


def over(value, by):
    return value // by if isinstance(value, int) else lax.div(value, by)


def rounds_of(lights, screens):
    per = screens // lights
    return [(step, core) for core in range(per) for step in range(lights)]


def target_screen(light, screen, rnd, lights, screens):
    per = screens // lights
    step, core = rnd
    return (bit_reversed(over(screen, per), lights) ^ light ^ step) * per + ((screen & (per - 1)) ^ core)


def source_of(light, screen, rnd, lights, screens):
    per = screens // lights
    step, core = rnd
    return bit_reversed(light, lights) ^ over(screen, per) ^ step, (screen & (per - 1)) ^ core


def round_pairs(rnd, lights, screens):
    per = screens // lights
    pairs = []
    for light in range(lights):
        for screen in range(screens):
            there = (screen // per) * screens + target_screen(light, screen, rnd, lights, screens)
            pairs.append((light * screens + screen, there))
    return pairs


def brick_rows(occ_ref, out, width):
    bricks = occ_ref.shape[1]
    here = lax.broadcasted_iota(jnp.int32, (bricks, width), 1) // BRICK
    spread = (here == lax.broadcasted_iota(jnp.int32, (bricks, width), 0)).astype(jnp.float32)
    flags = occ_ref[0].astype(jnp.float32)
    out[...] = lax.dot_general(flags, spread, (((0,), (0,)), ((), ())), preferred_element_type=jnp.float32)


def halves(values):
    high = values.astype(jnp.bfloat16)
    low = (values - high.astype(jnp.float32)).astype(jnp.bfloat16)
    return jnp.concatenate([high, low], axis=-1)


def prefix_matrix(width, with_total):
    rows = lax.broadcasted_iota(jnp.int32, (2 * width, (1 + with_total) * width), 0) % width
    cols = lax.broadcasted_iota(jnp.int32, (2 * width, (1 + with_total) * width), 1)
    return (rows < cols).astype(jnp.float32).astype(jnp.bfloat16)


def chunk_kernel(count, spot_of, first, has_small, *refs):
    occ_ref, density_ref, albedo_ref = refs[:3]
    outs = refs[3 + has_small : -3]
    small_ref, brick, tri = refs[-3:]
    step = pl.program_id(0)
    depth, rows, width = density_ref.shape

    @pl.when(step == 0)
    def _():
        brick_rows(occ_ref, brick, width)
        tri[...] = prefix_matrix(width, 1)

    bands = rows // BRICK
    spot = spot_of(first + step)
    mask = jnp.concatenate(
        [jnp.broadcast_to(brick[pl.ds(spot * bands + band, 1), :], (BRICK, width)) for band in range(bands)], axis=0
    )
    masked = (density_ref[...] * mask[None]).reshape(depth * rows, width)
    sums = jnp.dot(halves(masked), tri[...], preferred_element_type=jnp.float32)
    within = jnp.exp(-sums[:, :width])
    total = sums[:, width:]
    albedo = albedo_ref[...].reshape(depth * rows, width)
    lane = lax.broadcasted_iota(jnp.int32, (SUB, width), 1)
    packed = [jnp.zeros((SUB, width), jnp.float32)] * 3
    for b in range(depth):
        for group in range(rows // SUB):
            at = b * rows + group * SUB
            here = lane == group * depth + b
            packed[0] = jnp.where(here, total[at : at + SUB], packed[0])
            packed[1] = jnp.where(here, masked[at : at + SUB, 0:1], packed[1])
            packed[2] = jnp.where(here, albedo[at : at + SUB, 0:1], packed[2])
    for kind in range(3):
        small_ref[kind] = packed[kind]
    lit = albedo * within
    for index in range(count):

        @pl.when(step == index)
        def _():
            outs[index][: depth * rows, :] = lit
            outs[index][depth * rows :, :] = packed[0]


def lit_chunks(density, albedo, occupancy, spot_of, first, count, screens, small):
    depth, width_a, width = density.shape
    rows = width_a // screens
    spec = pl.BlockSpec((depth, rows, width), lambda i: (0, spot_of(first + i), 0))
    size = depth * rows + SUB
    has_small = small is not None
    return pl.pallas_call(
        functools.partial(chunk_kernel, count, spot_of, first, int(has_small)),
        grid=(count,),
        in_specs=[pl.BlockSpec(occupancy.shape, lambda i: (0, 0, 0)), spec, spec]
        + [pl.BlockSpec(memory_space=pl.ANY)] * has_small,
        out_specs=[pl.BlockSpec((size, width), lambda i: (0, 0))] * count
        + [pl.BlockSpec((3, SUB, width), lambda i: (0, spot_of(first + i), 0))],
        out_shape=[jax.ShapeDtypeStruct((size, width), jnp.float32)] * count
        + [jax.ShapeDtypeStruct((3, SUB * screens, width), jnp.float32)],
        scratch_shapes=[
            pltpu.VMEM((occupancy.shape[2], width), jnp.float32),
            pltpu.VMEM((2 * width, 2 * width), jnp.bfloat16),
        ],
        input_output_aliases={3: count} if has_small else {},
        compiler_params=pltpu.CompilerParams(vmem_limit_bytes=CHUNK_VMEM),
        cost_estimate=pl.CostEstimate(flops=10**7 * count, bytes_accessed=3 * size * width * 4 * count, transcendentals=0),
        name="lit_chunks",
    )(occupancy, density, albedo, *([small] if has_small else []))


CHUNK_VMEM = 56 << 20
MARCH_VMEM = 56 << 20


def gather_kernel(depth, lights, place_of, light_ref, *refs):
    count = len(refs) - 4
    chunks = refs[:count]
    out_ref, held, totals, sem = refs[count:]
    size, width = chunks[0].shape
    rows = (size - SUB) // depth
    for j in range(count):
        light, place = place_of(j)
        totals[place, light] = chunks[j][size - SUB :, :]
    copies = []
    for j in range(count):
        light, place = place_of(j)
        before = jnp.zeros((SUB, width), jnp.float32)
        for other in range(lights - 1):
            before = before + jnp.where(other < light, totals[place, other], 0.0)
        factor = light_ref[place] * jnp.exp(-before)
        for b in range(depth):
            for group in range(rows // SUB):
                at = b * rows + group * SUB
                lane = group * depth + b
                held[j, b, group * SUB : (group + 1) * SUB, :] = chunks[j][at : at + SUB, :] * factor[:, lane : lane + 1]
        copy = pltpu.make_async_copy(
            held.at[j],
            out_ref.at[pl.ds(place * depth, depth), :, pl.ds(pl.multiple_of(light * width, width), width)],
            sem.at[j],
        )
        copy.start()
        copies.append(copy)
    for copy in copies:
        copy.wait()


def gather_block(chunks, incoming, place_of, depth, lights, per):
    size, width = chunks[0].shape
    rows = (size - SUB) // depth
    return pl.pallas_call(
        functools.partial(gather_kernel, depth, lights, place_of),
        in_specs=[pl.BlockSpec(memory_space=pltpu.VMEM)] * (1 + len(chunks)),
        out_specs=pl.BlockSpec(memory_space=pl.ANY),
        out_shape=jax.ShapeDtypeStruct((per * depth, rows, lights * width), jnp.float32),
        scratch_shapes=[
            pltpu.VMEM((len(chunks), depth, rows, width), jnp.float32),
            pltpu.VMEM((per, lights, SUB, width), jnp.float32),
            pltpu.SemaphoreType.DMA((len(chunks),)),
        ],
        compiler_params=pltpu.CompilerParams(vmem_limit_bytes=24 << 20),
        name="gather_block",
    )(incoming, *chunks)


def march_kernel(
    lights, occ_ref, frac_ref, density_ref, albedo_ref, light_ref, small_ref, *refs
):
    others = refs[: lights - 1]
    phase_ref, first_ref, state_ref, weight_ref, brick, mask, columns, mixes, front, tri, field = refs[lights - 1 :]
    b = pl.program_id(0)
    depth = pl.num_programs(0)
    _, width_a, width = density_ref.shape
    steps = light_ref.shape[1]

    @pl.when(b == 0)
    def _():
        brick_rows(occ_ref, brick, width)
        for row in range(width_a // BRICK):
            mask[row * BRICK : (row + 1) * BRICK, :] = jnp.broadcast_to(brick[row : row + 1, :], (BRICK, width))
        levels = phase_ref[...]
        for axis in range(3):
            weight = jnp.zeros((width_a, width), jnp.float32)
            for level in range(frac_ref.shape[1]):
                weight = jnp.where(levels == level, frac_ref[axis, level], weight)
            weight_ref[axis] = weight
        tri[...] = prefix_matrix(width, 0)
        light = lax.axis_index("light")
        near = jnp.zeros(small_ref.shape[1:], jnp.float32)
        next_m = jnp.zeros(small_ref.shape[1:], jnp.float32)
        next_a = jnp.zeros(small_ref.shape[1:], jnp.float32)
        for by in range(1, lights):
            other = light ^ by
            near = near + jnp.where(other < light, others[by - 1][0], 0.0)
            next_m = next_m + jnp.where(other == light + 1, others[by - 1][1], 0.0)
            next_a = next_a + jnp.where(other == light + 1, others[by - 1][2], 0.0)
        far = jnp.exp(-(near + small_ref[0])) * next_a
        near = jnp.exp(-near)
        chunks = near.shape[0] // SUB
        groups = width_a // chunks // SUB
        pad = jnp.zeros((SUB, width - steps), jnp.float32)
        for chunk in range(chunks):
            for group in range(groups):
                at = (chunk * groups + group) * SUB
                back = (width - group * steps) % width

                def turned(x):
                    tile = x[chunk * SUB : (chunk + 1) * SUB]
                    return pltpu.roll(tile, back, 1) if back else tile

                incoming = jnp.concatenate([light_ref[at : at + SUB, :], pad], axis=1)
                columns[0, at : at + SUB, :] = incoming * turned(near)
                columns[1, at : at + SUB, :] = turned(next_m)
                columns[2, at : at + SUB, :] = incoming * turned(far)
        state_ref[...] = jnp.zeros_like(state_ref)
        front[...] = jnp.ones_like(front)
        mixes[...] = jnp.zeros_like(mixes)
        field[:, width_a:, :] = jnp.zeros((4, SUB, width), jnp.float32)

    lane = lax.broadcasted_iota(jnp.int32, (width_a, width), 1)
    masked = density_ref[0] * mask[...]
    within = jnp.dot(halves(masked), tri[...], preferred_element_type=jnp.float32)
    lit = albedo_ref[0] * columns[0][:, 0:1] * jnp.exp(-within)
    field[0, :width_a, :] = masked
    field[1, :width_a, :] = lit
    field[2, :width_a, :] = jnp.where(lane == width - 1, columns[1][:, 0:1], pltpu.roll(masked, width - 1, 1))
    field[3, :width_a, :] = jnp.where(lane == width - 1, columns[2][:, 0:1], pltpu.roll(lit, width - 1, 1))
    for kind in range(3):
        columns[kind] = pltpu.roll(columns[kind], width - 1, 1)

    for start in range(0, width_a, BAND):
        at = slice(start, start + BAND)
        below = slice(start + 1, start + BAND + 1)
        depth_w = weight_ref[0, at, :]
        column_w = weight_ref[1, at, :]
        light_w = weight_ref[2, at, :]

        def mixed(kind):
            near = field[kind, at, :]
            near = near + column_w * (field[kind, below, :] - near)
            after = field[kind + 2, at, :]
            after = after + column_w * (field[kind + 2, below, :] - after)
            return near + light_w * (after - near)

        mix_m = mixed(0)
        mix_s = mixed(1)
        old_m = mixes[0, at, :]
        old_s = mixes[1, at, :]
        extinct = old_m + depth_w * (mix_m - old_m)
        shaded = old_s + depth_w * (mix_s - old_s)
        extinct = jnp.where(b > 0, extinct, 0.0)
        total = state_ref[1, at, :] + extinct
        left = jnp.exp(-total)
        state_ref[0, at, :] = state_ref[0, at, :] + (front[at, :] - left) * shaded
        state_ref[1, at, :] = total
        front[at, :] = left
        mixes[0, at, :] = mix_m
        mixes[1, at, :] = mix_s

    @pl.when(b == 0)
    def _():
        first_ref[...] = mixes[...]

    @pl.when(b == depth - 1)
    def _():
        state_ref[2:] = mixes[...]


BAND = 64


def march(density, albedo, light_cols, occupancy, fractions, small, others, rays):
    depth, width_a, width = density.shape
    spec = pl.BlockSpec((1, width_a, width), lambda b: (b, 0, 0))

    def whole(x):
        return pl.BlockSpec(x.shape, lambda b: (0,) * x.ndim)

    shapes = [(2, width_a, width), (4, width_a, width), (3, width_a, width)]
    return pl.pallas_call(
        functools.partial(march_kernel, len(others) + 1),
        grid=(depth,),
        in_specs=[whole(occupancy), pl.BlockSpec(memory_space=pltpu.SMEM), spec, spec]
        + [whole(x) for x in (light_cols, small, *others, rays)],
        out_specs=[pl.BlockSpec(s, lambda b: (0, 0, 0)) for s in shapes],
        scratch_shapes=[
            pltpu.VMEM((occupancy.shape[2], width), jnp.float32),
            pltpu.VMEM((width_a, width), jnp.float32),
            pltpu.VMEM((3, width_a, width), jnp.float32),
            pltpu.VMEM((2, width_a, width), jnp.float32),
            pltpu.VMEM((width_a, width), jnp.float32),
            pltpu.VMEM((2 * width, width), jnp.bfloat16),
            pltpu.VMEM((4, width_a + SUB, width), jnp.float32),
        ],
        out_shape=[jax.ShapeDtypeStruct(s, jnp.float32) for s in shapes],
        compiler_params=pltpu.CompilerParams(vmem_limit_bytes=MARCH_VMEM),
        cost_estimate=pl.CostEstimate(flops=10**8, bytes_accessed=2 * depth * width_a * width * 4, transcendentals=0),
        name="march",
    )(occupancy, fractions, density, albedo, light_cols, small, *others, rays)


def shifted(value, axis, by):
    peers = lax.axis_size(axis)
    return lax.ppermute(value, axis, [(i, i + by) for i in range(peers) if 0 <= i + by < peers])


def swapped(value, axis, by):
    peers = lax.axis_size(axis)
    return lax.ppermute(value, axis, [(i, i ^ by) for i in range(peers)])


def step(density, albedo, light_in, occupancy, phase, fractions):
    depth, width_a, width = density.shape
    lights, screens = lax.axis_size("light"), lax.axis_size("screen")
    light, screen = lax.axis_index("light"), lax.axis_index("screen")
    per = screens // lights
    rows = width_a // screens
    rounds = rounds_of(lights, screens)
    pairs = [round_pairs(rnd, lights, screens) for rnd in rounds]

    def spot_of(j):
        here = lax.axis_index("light"), lax.axis_index("screen")
        return target_screen(*here, (lax.rem(j, lights), lax.div(j, lights)), lights, screens)

    def place_of(j):
        return source_of(lax.axis_index("light"), lax.axis_index("screen"), rounds[j], lights, screens)

    def send(j, chunk):
        return lax.ppermute(chunk, ("light", "screen"), pairs[j])

    count = len(rounds)
    flags = occupancy.transpose(0, 2, 1)
    early = lit_chunks(density, albedo, flags, spot_of, 0, 2, screens, None)
    late = lit_chunks(density, albedo, flags, spot_of, 2, count - 2, screens, early[-1])
    small = late[-1]
    arrived = [send(j, chunk) for j, chunk in enumerate(early[:2] + late[:-1])]

    others = [swapped(small, "light", by) for by in range(1, lights)]
    light_cols = lax.dynamic_slice_in_dim(light_in, screen * depth, depth, 0).T
    rays = lax.dynamic_slice_in_dim(phase, light * width, width, 1)
    first, state, weights = march(density, albedo, light_cols, flags, fractions, small, others, rays)
    behind = shifted(first, "screen", -1)
    extinct = state[2] + weights[0] * (behind[0] - state[2])
    shaded = state[3] + weights[0] * (behind[1] - state[3])
    total = state[1] + extinct
    part = state[0] + (jnp.exp(-state[1]) - jnp.exp(-total)) * shaded

    pair = jnp.stack([part, total]).reshape(2, screens // 2, 2, rows, width)
    core = screen % 2
    mine = lax.dynamic_index_in_dim(pair, core, 2, False)
    theirs = lax.dynamic_index_in_dim(pair, 1 - core, 2, False)
    other = swapped(theirs, "screen", 1)
    closer = jnp.where(core == 0, mine, other)
    farther = jnp.where(core == 0, other, mine)
    joined = jnp.stack([closer[0] + jnp.exp(-closer[1]) * farther[0], closer[1] + farther[1]])
    place = screen // 2
    got = [lax.dynamic_index_in_dim(joined, place, 1, False)]
    for by in range(1, screens // 2):
        piece = lax.dynamic_index_in_dim(joined, place ^ by, 1, False)
        got.append(swapped(piece, "screen", 2 * by))
    image = jnp.zeros((rows, width), jnp.float32)
    through = jnp.zeros((rows, width), jnp.float32)
    for by, (shine, thick) in enumerate(got):
        ahead = jnp.zeros((rows, width), jnp.float32)
        for other_by, (_, other_thick) in enumerate(got):
            if other_by != by:
                ahead = ahead + jnp.where((place ^ other_by) < (place ^ by), other_thick, 0.0)
        image = image + jnp.exp(-ahead) * shine
        through = through + thick
    incoming = lax.dynamic_slice(light_in, (light * per * depth, screen * rows), (per * depth, rows))
    incoming = incoming.reshape(per, depth, rows // SUB, SUB).transpose(0, 3, 2, 1).reshape(per, SUB, rows // SUB * depth)
    incoming = jnp.pad(incoming, ((0, 0), (0, 0), (0, width - incoming.shape[2])))
    lit_bricks = gather_block(arrived, incoming, place_of, depth, lights, per)
    return image, jnp.exp(-through), lit_bricks


def solution(mesh):
    return jax.shard_map(
        step,
        mesh=mesh,
        in_specs=(
            P("screen", None, "light"),
            P("screen", None, "light"),
            P(),
            P("screen", None, "light"),
            P(),
            P(),
        ),
        out_specs=(P("screen", "light"), P("screen", "light"), P("light", "screen", None)),
        check_vma=False,
    )
```

time: 197 us -> 109 us (0.55)
  the two profiles are of different devices: /device:TPU:0 before, /device:TPU:3 now
where the time goes in v1:
time: 109 us; the launch traced here: 108 us
  starting transfers between devices  56.6 us (52%)
  Pallas kernels  25.2 us (23%)
  waiting for transfers between devices  19.3 us (18%)
  local copies, waits for them, and re-layouts  3.86 us (4%)
  other arithmetic  2.57 us (2%)
    ppermute x7, starting transfers between devices, swapped(): return lax.ppermute(value, axis, [(i, i ^ by) for i in range(peers)])  32.3 us
    ppermute x8, starting transfers between devices, send(): return lax.ppermute(chunk, ('light', 'screen'), pairs[j])  20.8 us
    pallas_call x1, Pallas kernels, march(): pl.pallas_call(functools.partial(march_kernel, len(others) + 1), grid=(de...  14.4 us
    ppermute x8, waiting for transfers between devices, send(): return lax.ppermute(chunk, ('light', 'screen'), pairs[j])  11.5 us
    pallas_call x2, Pallas kernels, lit_chunks(): pl.pallas_call(functools.partial(chunk_kernel, count, spot_of, first, int...  9 us
    ppermute x1, waiting for transfers between devices, shifted(): lax.ppermute(value, axis, [(i, i + by) for i in range(peers) if 0 <= i +...  5.42 us
    ppermute x1, starting transfers between devices, shifted(): lax.ppermute(value, axis, [(i, i + by) for i in range(peers) if 0 <= i +...  3.42 us
    ppermute x7, waiting for transfers between devices, swapped(): return lax.ppermute(value, axis, [(i, i ^ by) for i in range(peers)])  2.38 us
  transfers between devices with their start and end apart: 16, of which 4 were waited for; matrix products, arithmetic and copies ran while one was open for 3% of the time, Pallas kernels for 2%

profile of v1, /device:TPU:3, one launch (start us, length us, event | category | flops | bytes accessed | tf_op | source)
XLA Modules:
  0.0 108.4 jit_solution(10545568227288726051)
XLA Ops:
  0.6 2.8 %lit_chunks.2 = (f32[520,128]{1,0:T(8,128)}, f32[520,128]{1,0:T(8,128)}, f32[3,64,128]{2,1,0:T(8,128)}) custom-call(s32[1,8,16]{2,1,0:T(8,128)} %bitcast.79, f32[16,256,128]{2,1,0:T(8,128)} %density_ref.1, f32[16,256,128]{2,1,0:T(8,128)} %albedo_ref.1), custom_call_target="tpu_custom_call" | custom-call | flops 20000000 | bytes 1597440 | tf_op jit(solution)/shard_map/lit_chunks/pallas_call | solution.py:123
  3.4 6.2 %lit_chunks.3 = (f32[520,128]{1,0:T(8,128)}, f32[520,128]{1,0:T(8,128)}, f32[520,128]{1,0:T(8,128)}, f32[520,128]{1,0:T(8,128)}, f32[520,128]{1,0:T(8,128)}, /*index=5*/f32[520,128]{1,0:T(8,128)}, f32[3,64,128]{2,1,0:T(8,128)}) custom-call(s32[1,8,16]{2,1,0:T(8,128)} %bitcast.80, f32[16,256,128]{2,1,0:T(8,128)} %density_ref.1, ...), custom_call_target="tpu_custom_call", output_to_operand_aliasing={{6}: (3, {})} | custom-call | flops 60000000 | bytes 4792320 | tf_op jit(solution)/shard_map/lit_chunks/pallas_call | solution.py:123
  9.7 1.5 %collective-permute-start.1 = (f32[3,64,128]{2,1,0:T(8,128)}, f32[3,64,128]{2,1,0:T(8,128)S(1)}, u32[]{:S(2)}, u32[]{:S(2)}) collective-permute-start(f32[3,64,128]{2,1,0:T(8,128)} %get-tuple-element.17.small_ref), channel_id=1, source_target_pairs={{0,16},{8,24},{16,0},{24,8},{1,17},{9,25},{17,1},{25,9},{2,18},{10... | collective-permute-start | bytes 294920 | tf_op jit(solution)/shard_map/ppermute | solution.py:340
  11.2 1.2 %collective-permute-start.2 = (f32[3,64,128]{2,1,0:T(8,128)}, f32[3,64,128]{2,1,0:T(8,128)S(1)}, u32[]{:S(2)}, u32[]{:S(2)}) collective-permute-start(f32[3,64,128]{2,1,0:T(8,128)} %get-tuple-element.17.small_ref), channel_id=1, source_target_pairs={{0,24},{8,16},{16,8},{24,0},{1,25},{9,17},{17,9},{25,1},{2,26},{10... | collective-permute-start | bytes 294920 | tf_op jit(solution)/shard_map/ppermute | solution.py:340
  12.3 0.7 constant_dynamic-slice_fusion.1
  13.0 0.8 copy.14
  13.8 0.7 constant_dynamic-slice_fusion.refs_3_
  14.5 2.4 %collective-permute-done.2.refs_2_ = f32[3,64,128]{2,1,0:T(8,128)S(1)} collective-permute-done((f32[3,64,128]{2,1,0:T(8,128)}, f32[3,64,128]{2,1,0:T(8,128)S(1)}, u32[]{:S(2)}, u32[]{:S(2)}) %collective-permute-start.2) | collective-permute-done | bytes 98336 | tf_op jit(solution)/shard_map/ppermute | solution.py:340
  16.9 0.6 copy-done.3
  17.5 14.4 %march.1 = (f32[2,256,128]{2,1,0:T(8,128)}, f32[4,256,128]{2,1,0:T(8,128)}, f32[3,256,128]{2,1,0:T(8,128)}) custom-call(s32[1,8,16]{2,1,0:T(8,128)} %bitcast.81, f32[3,16]{1,0:T(4,128)} %frac_ref.1, f32[16,256,128]{2,1,0:T(8,128)} %density_ref.1, f32[16,256,128]{2,1,0:T(8,128)} %albedo_ref.1, f32[256,16]{1,0:T(8,128)} %bitcast.77, ...), custom_call_target="tpu_custom_call" | custom-call | flops 100000000 | bytes 4194304 | tf_op jit(solution)/shard_map/march/pallas_call | solution.py:311
  31.9 3.4 %collective-permute-start.3 = (f32[2,256,128]{2,1,0:T(8,128)}, f32[2,256,128]{2,1,0:T(8,128)S(1)}, u32[]{:S(2)}, u32[]{:S(2)}) collective-permute-start(f32[2,256,128]{2,1,0:T(8,128)} %get-tuple-element.20), channel_id=1, source_target_pairs={{1,0},{2,1},{3,2},{4,3},{5,4},{6,5},{7,6},{9,8},{10,9},{11,10},{12... | collective-permute-start | bytes 786440 | tf_op jit(solution)/shard_map/ppermute | solution.py:335
  35.4 5.4 %collective-permute-done.3 = f32[2,256,128]{2,1,0:T(8,128)S(1)} collective-permute-done((f32[2,256,128]{2,1,0:T(8,128)}, f32[2,256,128]{2,1,0:T(8,128)S(1)}, u32[]{:S(2)}, u32[]{:S(2)}) %collective-permute-start.3) | collective-permute-done | bytes 262176 | tf_op jit(solution)/shard_map/ppermute | solution.py:335
  40.8 1.2 %fusion.7 = (f32[1,256,128]{2,1,0:T(8,128)S(1)}, f32[1,256,128]{2,1,0:T(8,128)S(1)}) fusion(f32[2,256,128]{2,1,0:T(8,128)S(1)} %collective-permute-done.3, f32[4,256,128]{2,1,0:T(8,128)} %get-tuple-element.18, f32[3,256,128]{2,1,0:T(8,128)} %get-tuple-element.19), kind=kLoop, calls=%fused_computation.20 | loop fusion | flops 393216 | bytes 1179648 | tf_op jit(solution)/shard_map/add | solution.py:377
  42.1 4.8 %collective-permute-start.10 = (f32[520,128]{1,0:T(8,128)}, f32[520,128]{1,0:T(8,128)S(1)}, u32[]{:S(2)}, u32[]{:S(2)}) collective-permute-start(f32[520,128]{1,0:T(8,128)} %get-tuple-element.23), channel_id=1, source_target_pairs={{0,4},{1,5},{2,8},{3,9},{4,22},{5,23},{6,26},{7,27},{8,6},{9,7},{1... | collective-permute-start | bytes 798728 | tf_op jit(solution)/shard_map/ppermute | solution.py:360
  46.9 2.6 %collective-permute-start.11 = (f32[520,128]{1,0:T(8,128)S(1)}, f32[520,128]{1,0:T(8,128)S(1)}, u32[]{:S(2)}, u32[]{:S(2)}) collective-permute-start(f32[520,128]{1,0:T(8,128)S(1)} %copy-done.7), channel_id=1, source_target_pairs={{0,6},{1,7},{2,10},{3,11},{4,20},{5,21},{6,24},{7,25},{8,4},{9,5},... | collective-permute-start | bytes 798728 | tf_op jit(solution)/shard_map/ppermute | solution.py:360
  49.6 2.4 %collective-permute-start.13 = (f32[520,128]{1,0:T(8,128)}, f32[520,128]{1,0:T(8,128)S(1)}, u32[]{:S(2)}, u32[]{:S(2)}) collective-permute-start(f32[520,128]{1,0:T(8,128)} %get-tuple-element.26), channel_id=1, source_target_pairs={{0,3},{1,2},{2,15},{3,14},{4,17},{5,16},{6,29},{7,28},{8,1},{9,0},... | collective-permute-start | bytes 798728 | tf_op jit(solution)/shard_map/ppermute | solution.py:360
  52.0 2.3 %collective-permute-start.14 = (f32[520,128]{1,0:T(8,128)}, f32[520,128]{1,0:T(8,128)S(1)}, u32[]{:S(2)}, u32[]{:S(2)}) collective-permute-start(f32[520,128]{1,0:T(8,128)} %get-tuple-element.27), channel_id=1, source_target_pairs={{0,5},{1,4},{2,9},{3,8},{4,23},{5,22},{6,27},{7,26},{8,7},{9,6},{1... | collective-permute-start | bytes 798728 | tf_op jit(solution)/shard_map/ppermute | solution.py:360
  54.4 4.8 %collective-permute-start.15 = (f32[520,128]{1,0:T(8,128)}, f32[520,128]{1,0:T(8,128)S(1)}, u32[]{:S(2)}, u32[]{:S(2)}) collective-permute-start(f32[520,128]{1,0:T(8,128)} %get-tuple-element.28), channel_id=1, source_target_pairs={{0,7},{1,6},{2,11},{3,10},{4,21},{5,20},{6,25},{7,24},{8,5},{9,4},... | collective-permute-start | bytes 798728 | tf_op jit(solution)/shard_map/ppermute | solution.py:360
  59.2 3.1 %collective-permute-done.11.refs_3_ = f32[520,128]{1,0:T(8,128)S(1)} collective-permute-done((f32[520,128]{1,0:T(8,128)S(1)}, f32[520,128]{1,0:T(8,128)S(1)}, u32[]{:S(2)}, u32[]{:S(2)}) %collective-permute-start.11) | collective-permute-done | bytes 266272 | tf_op jit(solution)/shard_map/ppermute | solution.py:360
  62.3 1.9 %collective-permute-start.8 = (f32[520,128]{1,0:T(8,128)S(1)}, f32[520,128]{1,0:T(8,128)S(1)}, u32[]{:S(2)}, u32[]{:S(2)}) collective-permute-start(f32[520,128]{1,0:T(8,128)S(1)} %copy-done.5), channel_id=1, source_target_pairs={{0,0},{1,1},{2,12},{3,13},{4,18},{5,19},{6,30},{7,31},{8,2},{9,3},... | collective-permute-start | bytes 798728 | tf_op jit(solution)/shard_map/ppermute | solution.py:360
  64.2 8.4 %collective-permute-done.12.refs_4_ = f32[520,128]{1,0:T(8,128)S(1)} collective-permute-done((f32[520,128]{1,0:T(8,128)S(1)}, f32[520,128]{1,0:T(8,128)S(1)}, u32[]{:S(2)}, u32[]{:S(2)}) %collective-permute-start.12) | collective-permute-done | bytes 266272 | tf_op jit(solution)/shard_map/ppermute | solution.py:360
  72.6 1.9 %collective-permute-start.9 = (f32[520,128]{1,0:T(8,128)S(1)}, f32[520,128]{1,0:T(8,128)S(1)}, u32[]{:S(2)}, u32[]{:S(2)}) collective-permute-start(f32[520,128]{1,0:T(8,128)S(1)} %copy-done.4), channel_id=1, source_target_pairs={{0,2},{1,3},{2,14},{3,15},{4,16},{5,17},{6,28},{7,29},{8,0},{9,1},... | collective-permute-start | bytes 798728 | tf_op jit(solution)/shard_map/ppermute | solution.py:360
  74.6 8.7 %collective-permute-start.5 = (f32[2,32,128]{2,1,0:T(8,128)S(1)}, f32[2,32,128]{2,1,0:T(8,128)S(1)}, u32[]{:S(2)}, u32[]{:S(2)}) collective-permute-start(f32[2,32,128]{2,1,0:T(8,128)S(1)} %get-tuple-element.36), channel_id=1, source_target_pairs={{0,2},{1,3},{2,0},{3,1},{4,6},{5,7},{6,4},{7,5},{8,10},{9,11},{10,... | collective-permute-start | bytes 98312 | tf_op jit(solution)/shard_map/ppermute | solution.py:340
  83.3 5.0 %collective-permute-start.6 = (f32[2,32,128]{2,1,0:T(8,128)S(1)}, f32[2,32,128]{2,1,0:T(8,128)S(1)}, u32[]{:S(2)}, u32[]{:S(2)}) collective-permute-start(f32[2,32,128]{2,1,0:T(8,128)S(1)} %get-tuple-element.37), channel_id=1, source_target_pairs={{0,4},{1,5},{2,6},{3,7},{4,0},{5,1},{6,2},{7,3},{8,12},{9,13},{10,... | collective-permute-start | bytes 98312 | tf_op jit(solution)/shard_map/ppermute | solution.py:340
  88.3 15.9 %collective-permute-start.7 = (f32[2,32,128]{2,1,0:T(8,128)S(1)}, f32[2,32,128]{2,1,0:T(8,128)S(1)}, u32[]{:S(2)}, u32[]{:S(2)}) collective-permute-start(f32[2,32,128]{2,1,0:T(8,128)S(1)} %get-tuple-element.38), channel_id=1, source_target_pairs={{0,6},{1,7},{2,4},{3,5},{4,2},{5,3},{6,0},{7,1},{8,14},{9,15},{10,... | collective-permute-start | bytes 98312 | tf_op jit(solution)/shard_map/ppermute | solution.py:340
  104.1 0.8 dynamic_slice.37
  104.9 0.1 copy.12
  105.0 0.1 reshape.19
  105.1 0.1 reshape.20
  105.2 1.8 %gather_block.1 = f32[32,32,512]{2,1,0:T(8,128)} custom-call(f32[2,8,128]{2,1,0:T(8,128)S(1)} %pad.4.light_ref, f32[520,128]{1,0:T(8,128)S(1)} %collective-permute-done.8.refs_0_, f32[520,128]{1,0:T(8,128)S(1)} %collective-permute-done.9.refs_1_, f32[520,128]{1,0:T(8,128)S(1)} %collective-permute-done.10.refs_2_, ...), custom_call_target="tpu_custom_call" | custom-call | tf_op jit(solution)/shard_map/gather_block/pallas_call | solution.py:182
  107.1 0.6 negate_exponential_fusion
  107.7 0.6 fusion.20
  (36 shorter events, 0.3 us)
Async XLA Ops:
  0.6 13.2 %copy-start = (s32[256,512]{1,0:T(8,128)S(1)}, s32[256,512]{1,0:T(8,128)}, u32[]{:S(2)}) copy-start(s32[256,512]{1,0:T(8,128)} %param.10) | copy-start | bytes 1572868
  9.6 4.8 %collective-permute-start = (f32[3,64,128]{2,1,0:T(8,128)}, f32[3,64,128]{2,1,0:T(8,128)S(1)}, u32[]{:S(2)}, u32[]{:S(2)}) collective-permute-start(f32[3,64,128]{2,1,0:T(8,128)} %get-tuple-element.17.small_ref), channel_id=1, source_target_pairs={{0,8},{8,0},{16,24},{24,16},{1,9},{9,1},{17,25},{25,17},{2,10},{10... | collective-permute-start | bytes 294920 | tf_op jit(solution)/shard_map/ppermute | solution.py:340
  9.7 4.8 %collective-permute-start.1 = (f32[3,64,128]{2,1,0:T(8,128)}, f32[3,64,128]{2,1,0:T(8,128)S(1)}, u32[]{:S(2)}, u32[]{:S(2)}) collective-permute-start(f32[3,64,128]{2,1,0:T(8,128)} %get-tuple-element.17.small_ref), channel_id=1, source_target_pairs={{0,16},{8,24},{16,0},{24,8},{1,17},{9,25},{17,1},{25,9},{2,18},{10... | collective-permute-start | bytes 294920 | tf_op jit(solution)/shard_map/ppermute | solution.py:340
  11.2 5.7 %collective-permute-start.2 = (f32[3,64,128]{2,1,0:T(8,128)}, f32[3,64,128]{2,1,0:T(8,128)S(1)}, u32[]{:S(2)}, u32[]{:S(2)}) collective-permute-start(f32[3,64,128]{2,1,0:T(8,128)} %get-tuple-element.17.small_ref), channel_id=1, source_target_pairs={{0,24},{8,16},{16,8},{24,0},{1,25},{9,17},{17,9},{25,1},{2,26},{10... | collective-permute-start | bytes 294920 | tf_op jit(solution)/shard_map/ppermute | solution.py:340
  14.5 2.4 %copy-start.1 = (f32[3,64,128]{2,1,0:T(8,128)}, f32[3,64,128]{2,1,0:T(8,128)S(1)}, u32[]{:S(2)}) copy-start(f32[3,64,128]{2,1,0:T(8,128)S(1)} %collective-permute-done.refs_0_) | copy-start | bytes 294916
  14.5 2.4 %copy-start.2 = (f32[3,64,128]{2,1,0:T(8,128)}, f32[3,64,128]{2,1,0:T(8,128)S(1)}, u32[]{:S(2)}) copy-start(f32[3,64,128]{2,1,0:T(8,128)S(1)} %collective-permute-done.1.refs_1_) | copy-start | bytes 294916
  16.9 0.6 copy-start.3
  17.5 29.4 %copy-start.7 = (f32[520,128]{1,0:T(8,128)S(1)}, f32[520,128]{1,0:T(8,128)}, u32[]{:S(2)}) copy-start(f32[520,128]{1,0:T(8,128)} %get-tuple-element.24) | copy-start | bytes 798724
  17.5 32.0 %copy-start.6 = (f32[520,128]{1,0:T(8,128)S(1)}, f32[520,128]{1,0:T(8,128)}, u32[]{:S(2)}) copy-start(f32[520,128]{1,0:T(8,128)} %get-tuple-element.25) | copy-start | bytes 798724
  31.9 30.4 %copy-start.5 = (f32[520,128]{1,0:T(8,128)S(1)}, f32[520,128]{1,0:T(8,128)}, u32[]{:S(2)}) copy-start(f32[520,128]{1,0:T(8,128)} %get-tuple-element.21) | copy-start | bytes 798724
  31.9 40.7 %copy-start.4 = (f32[520,128]{1,0:T(8,128)S(1)}, f32[520,128]{1,0:T(8,128)}, u32[]{:S(2)}) copy-start(f32[520,128]{1,0:T(8,128)} %get-tuple-element.22) | copy-start | bytes 798724
  31.9 8.9 %collective-permute-start.3 = (f32[2,256,128]{2,1,0:T(8,128)}, f32[2,256,128]{2,1,0:T(8,128)S(1)}, u32[]{:S(2)}, u32[]{:S(2)}) collective-permute-start(f32[2,256,128]{2,1,0:T(8,128)} %get-tuple-element.20), channel_id=1, source_target_pairs={{1,0},{2,1},{3,2},{4,3},{5,4},{6,5},{7,6},{9,8},{10,9},{11,10},{12... | collective-permute-start | bytes 786440 | tf_op jit(solution)/shard_map/ppermute | solution.py:335
  42.0 10.0 %collective-permute-start.4 = (f32[2,4,32,128]{3,2,1,0:T(8,128)S(1)}, f32[2,4,32,128]{3,2,1,0:T(8,128)S(1)}, u32[]{:S(2)}, u32[]{:S(2)}) collective-permute-start(f32[2,4,32,128]{3,2,1,0:T(8,128)S(1)} %fusion.1), channel_id=1, source_target_pairs={{0,1},{1,0},{2,3},{3,2},{4,5},{5,4},{6,7},{7,6},{8,9},{9,8},{10,11... | collective-permute-start | bytes 393224 | tf_op jit(solution)/shard_map/ppermute | solution.py:340
  42.1 12.3 %collective-permute-start.10 = (f32[520,128]{1,0:T(8,128)}, f32[520,128]{1,0:T(8,128)S(1)}, u32[]{:S(2)}, u32[]{:S(2)}) collective-permute-start(f32[520,128]{1,0:T(8,128)} %get-tuple-element.23), channel_id=1, source_target_pairs={{0,4},{1,5},{2,8},{3,9},{4,22},{5,23},{6,26},{7,27},{8,6},{9,7},{1... | collective-permute-start | bytes 798728 | tf_op jit(solution)/shard_map/ppermute | solution.py:360
  46.9 15.4 %collective-permute-start.11 = (f32[520,128]{1,0:T(8,128)S(1)}, f32[520,128]{1,0:T(8,128)S(1)}, u32[]{:S(2)}, u32[]{:S(2)}) collective-permute-start(f32[520,128]{1,0:T(8,128)S(1)} %copy-done.7), channel_id=1, source_target_pairs={{0,6},{1,7},{2,10},{3,11},{4,20},{5,21},{6,24},{7,25},{8,4},{9,5},... | collective-permute-start | bytes 798728 | tf_op jit(solution)/shard_map/ppermute | solution.py:360
  49.5 23.1 %collective-permute-start.12 = (f32[520,128]{1,0:T(8,128)S(1)}, f32[520,128]{1,0:T(8,128)S(1)}, u32[]{:S(2)}, u32[]{:S(2)}) collective-permute-start(f32[520,128]{1,0:T(8,128)S(1)} %copy-done.6), channel_id=1, source_target_pairs={{0,1},{1,0},{2,13},{3,12},{4,19},{5,18},{6,31},{7,30},{8,3},{9,2},... | collective-permute-start | bytes 798728 | tf_op jit(solution)/shard_map/ppermute | solution.py:360
  49.6 25.0 %collective-permute-start.13 = (f32[520,128]{1,0:T(8,128)}, f32[520,128]{1,0:T(8,128)S(1)}, u32[]{:S(2)}, u32[]{:S(2)}) collective-permute-start(f32[520,128]{1,0:T(8,128)} %get-tuple-element.26), channel_id=1, source_target_pairs={{0,3},{1,2},{2,15},{3,14},{4,17},{5,16},{6,29},{7,28},{8,1},{9,0},... | collective-permute-start | bytes 798728 | tf_op jit(solution)/shard_map/ppermute | solution.py:360
  52.0 31.3 %collective-permute-start.14 = (f32[520,128]{1,0:T(8,128)}, f32[520,128]{1,0:T(8,128)S(1)}, u32[]{:S(2)}, u32[]{:S(2)}) collective-permute-start(f32[520,128]{1,0:T(8,128)} %get-tuple-element.27), channel_id=1, source_target_pairs={{0,5},{1,4},{2,9},{3,8},{4,23},{5,22},{6,27},{7,26},{8,7},{9,6},{1... | collective-permute-start | bytes 798728 | tf_op jit(solution)/shard_map/ppermute | solution.py:360
  54.4 33.9 %collective-permute-start.15 = (f32[520,128]{1,0:T(8,128)}, f32[520,128]{1,0:T(8,128)S(1)}, u32[]{:S(2)}, u32[]{:S(2)}) collective-permute-start(f32[520,128]{1,0:T(8,128)} %get-tuple-element.28), channel_id=1, source_target_pairs={{0,7},{1,6},{2,11},{3,10},{4,21},{5,20},{6,25},{7,24},{8,5},{9,4},... | collective-permute-start | bytes 798728 | tf_op jit(solution)/shard_map/ppermute | solution.py:360
  62.3 42.9 %collective-permute-start.8 = (f32[520,128]{1,0:T(8,128)S(1)}, f32[520,128]{1,0:T(8,128)S(1)}, u32[]{:S(2)}, u32[]{:S(2)}) collective-permute-start(f32[520,128]{1,0:T(8,128)S(1)} %copy-done.5), channel_id=1, source_target_pairs={{0,0},{1,1},{2,12},{3,13},{4,18},{5,19},{6,30},{7,31},{8,2},{9,3},... | collective-permute-start | bytes 798728 | tf_op jit(solution)/shard_map/ppermute | solution.py:360
  72.6 32.6 %collective-permute-start.9 = (f32[520,128]{1,0:T(8,128)S(1)}, f32[520,128]{1,0:T(8,128)S(1)}, u32[]{:S(2)}, u32[]{:S(2)}) collective-permute-start(f32[520,128]{1,0:T(8,128)S(1)} %copy-done.4), channel_id=1, source_target_pairs={{0,2},{1,3},{2,14},{3,15},{4,16},{5,17},{6,28},{7,29},{8,0},{9,1},... | collective-permute-start | bytes 798728 | tf_op jit(solution)/shard_map/ppermute | solution.py:360
  74.6 32.5 %collective-permute-start.5 = (f32[2,32,128]{2,1,0:T(8,128)S(1)}, f32[2,32,128]{2,1,0:T(8,128)S(1)}, u32[]{:S(2)}, u32[]{:S(2)}) collective-permute-start(f32[2,32,128]{2,1,0:T(8,128)S(1)} %get-tuple-element.36), channel_id=1, source_target_pairs={{0,2},{1,3},{2,0},{3,1},{4,6},{5,7},{6,4},{7,5},{8,10},{9,11},{10,... | collective-permute-start | bytes 98312 | tf_op jit(solution)/shard_map/ppermute | solution.py:340
  83.3 23.8 %collective-permute-start.6 = (f32[2,32,128]{2,1,0:T(8,128)S(1)}, f32[2,32,128]{2,1,0:T(8,128)S(1)}, u32[]{:S(2)}, u32[]{:S(2)}) collective-permute-start(f32[2,32,128]{2,1,0:T(8,128)S(1)} %get-tuple-element.37), channel_id=1, source_target_pairs={{0,4},{1,5},{2,6},{3,7},{4,0},{5,1},{6,2},{7,3},{8,12},{9,13},{10,... | collective-permute-start | bytes 98312 | tf_op jit(solution)/shard_map/ppermute | solution.py:340
  88.3 18.8 %collective-permute-start.7 = (f32[2,32,128]{2,1,0:T(8,128)S(1)}, f32[2,32,128]{2,1,0:T(8,128)S(1)}, u32[]{:S(2)}, u32[]{:S(2)}) collective-permute-start(f32[2,32,128]{2,1,0:T(8,128)S(1)} %get-tuple-element.38), channel_id=1, source_target_pairs={{0,6},{1,7},{2,4},{3,5},{4,2},{5,3},{6,0},{7,1},{8,14},{9,15},{10,... | collective-permute-start | bytes 98312 | tf_op jit(solution)/shard_map/ppermute | solution.py:340

commit v2 on v1

v2 whole, which is shorter than its diff:
```python
import functools

import jax
import jax.numpy as jnp
from jax import lax
from jax.experimental import pallas as pl
from jax.experimental.pallas import tpu as pltpu
from jax.sharding import PartitionSpec as P


BRICK = 16
SUB = 8


def bit_reversed(value, size):
    out = 0
    bit = 1
    while bit < size:
        out = out * 2 + ((value // bit) & 1 if isinstance(value, int) else lax.div(value, bit) & 1)
        bit *= 2
    return out


def over(value, by):
    return value // by if isinstance(value, int) else lax.div(value, by)


def rounds_of(lights, screens):
    per = screens // lights
    return [(step, core) for core in range(per) for step in range(lights)]


def target_screen(light, screen, rnd, lights, screens):
    per = screens // lights
    step, core = rnd
    return (bit_reversed(over(screen, per), lights) ^ light ^ step) * per + ((screen & (per - 1)) ^ core)


def source_of(light, screen, rnd, lights, screens):
    per = screens // lights
    step, core = rnd
    return bit_reversed(light, lights) ^ over(screen, per) ^ step, (screen & (per - 1)) ^ core


def round_pairs(rnd, lights, screens):
    per = screens // lights
    pairs = []
    for light in range(lights):
        for screen in range(screens):
            there = (screen // per) * screens + target_screen(light, screen, rnd, lights, screens)
            pairs.append((light * screens + screen, there))
    return pairs


def brick_rows(occ_ref, out, width):
    bricks = occ_ref.shape[1]
    here = lax.broadcasted_iota(jnp.int32, (bricks, width), 1) // BRICK
    spread = (here == lax.broadcasted_iota(jnp.int32, (bricks, width), 0)).astype(jnp.float32)
    flags = occ_ref[0].astype(jnp.float32)
    out[...] = lax.dot_general(flags, spread, (((0,), (0,)), ((), ())), preferred_element_type=jnp.float32)


def halves(values):
    high = values.astype(jnp.bfloat16)
    low = (values - high.astype(jnp.float32)).astype(jnp.bfloat16)
    return jnp.concatenate([high, low], axis=-1)


def prefix_matrix(width, with_total):
    rows = lax.broadcasted_iota(jnp.int32, (2 * width, (1 + with_total) * width), 0) % width
    cols = lax.broadcasted_iota(jnp.int32, (2 * width, (1 + with_total) * width), 1)
    return (rows < cols).astype(jnp.float32).astype(jnp.bfloat16)


def chunk_kernel(count, spot_of, first, *refs):
    occ_any, density_ref, albedo_ref = refs[:3]
    before = refs[3 : 3 + bool(first)]
    rest = refs[3 + bool(first) :]
    outs = rest[:count]
    brims = rest[count : -7]
    small_ref, occ_ref, brick, tri, density, albedo, sem = rest[-7:]
    _, depth, rows, width = density.shape

    def fetches(k):
        columns = pl.ds(spot_of(first + k) * rows, rows)
        return (
            pltpu.make_async_copy(density_ref.at[:, columns, :], density.at[k], sem.at[0, k]),
            pltpu.make_async_copy(albedo_ref.at[:, columns, :], albedo.at[k], sem.at[1, k]),
        )

    flags = pltpu.make_async_copy(occ_any, occ_ref, sem.at[2, 0])
    flags.start()
    for k in range(count):
        for fetch in fetches(k):
            fetch.start()
    for brim in brims:
        pltpu.make_async_copy(density_ref.at[0], brim.at[0], sem.at[2, 1]).start()
        pltpu.make_async_copy(albedo_ref.at[0], brim.at[1], sem.at[2, 2]).start()
    tri[...] = prefix_matrix(width, 1)
    flags.wait()
    brick_rows(occ_ref, brick, width)
    bands = rows // BRICK
    lane = lax.broadcasted_iota(jnp.int32, (SUB, width), 1)
    for k in range(count):
        spot = spot_of(first + k)
        mask = jnp.concatenate(
            [jnp.broadcast_to(brick[pl.ds(spot * bands + band, 1), :], (BRICK, width)) for band in range(bands)], axis=0
        )
        for fetch in fetches(k):
            fetch.wait()
        packed = [jnp.zeros((SUB, width), jnp.float32)] * 3
        for b in range(depth):
            masked = density[k, b] * mask
            sums = jnp.dot(halves(masked), tri[...], preferred_element_type=jnp.float32)
            light = albedo[k, b]
            outs[k][b * rows : (b + 1) * rows, :] = light * jnp.exp(-sums[:, :width])
            for group in range(rows // SUB):
                at = slice(group * SUB, (group + 1) * SUB)
                here = lane == group * (depth + 1) + b
                packed[0] = jnp.where(here, sums[at, width:], packed[0])
                packed[1] = jnp.where(here, masked[at, 0:1], packed[1])
                packed[2] = jnp.where(here, light[at, 0:1], packed[2])
        outs[k][depth * rows :, :] = packed[0]
        tile = pl.multiple_of(spot * SUB, SUB) if first else k * SUB
        for kind in range(3):
            small_ref[kind, pl.ds(tile, SUB), :] = packed[kind]
    for brim in brims:
        pltpu.make_async_copy(density_ref.at[0], brim.at[0], sem.at[2, 1]).wait()
        pltpu.make_async_copy(albedo_ref.at[0], brim.at[1], sem.at[2, 2]).wait()
        for row in range(brick.shape[0]):
            at = slice(row * BRICK, (row + 1) * BRICK)
            brim[0, at, :] = brim[0, at, :] * brick[row : row + 1, :]
    for held in before:
        for k in range(first):
            tile = pl.multiple_of(spot_of(k) * SUB, SUB)
            small_ref[:, pl.ds(tile, SUB), :] = held[:, k * SUB : (k + 1) * SUB, :]


def lit_chunks(density, albedo, occupancy, spot_of, first, count, screens, *before):
    depth, width_a, width = density.shape
    rows = width_a // screens
    size = depth * rows + SUB
    vmem = pl.BlockSpec(memory_space=pltpu.VMEM)
    tiles = screens if before else count
    brim = [] if before else [jax.ShapeDtypeStruct((2, width_a, width), jnp.float32)]
    return pl.pallas_call(
        functools.partial(chunk_kernel, count, spot_of, first),
        in_specs=[pl.BlockSpec(memory_space=pl.ANY)] * 3 + [vmem] * len(before),
        out_specs=[vmem] * (count + 1 + len(brim)),
        out_shape=[jax.ShapeDtypeStruct((size, width), jnp.float32)] * count
        + brim
        + [jax.ShapeDtypeStruct((3, SUB * tiles, width), jnp.float32)],
        scratch_shapes=[
            pltpu.VMEM(occupancy.shape, occupancy.dtype),
            pltpu.VMEM((occupancy.shape[2], width), jnp.float32),
            pltpu.VMEM((2 * width, 2 * width), jnp.bfloat16),
            pltpu.VMEM((count, depth, rows, width), jnp.float32),
            pltpu.VMEM((count, depth, rows, width), jnp.float32),
            pltpu.SemaphoreType.DMA((3, max(count, 3))),
        ],
        compiler_params=pltpu.CompilerParams(vmem_limit_bytes=CHUNK_VMEM),
        cost_estimate=pl.CostEstimate(flops=10**7 * count, bytes_accessed=3 * size * width * 4 * count, transcendentals=0),
        name="lit_chunks",
    )(occupancy, density, albedo, *before)


CHUNK_VMEM = 12 << 20
MARCH_VMEM = 16 << 20


def rim_kernel(depth, small_ref, brim_ref, out_ref):
    _, width_a, width = brim_ref.shape
    tiles = small_ref.shape[1] // SUB
    groups = width_a // tiles // SUB
    masked = brim_ref[0]
    light = brim_ref[1]
    total = jnp.dot(halves(masked), jnp.ones((2 * width, width), jnp.bfloat16), preferred_element_type=jnp.float32)
    lane = lax.broadcasted_iota(jnp.int32, (SUB, width), 1)
    for tile in range(tiles):
        rows = slice(tile * SUB, (tile + 1) * SUB)
        packed = [small_ref[kind, rows, :] for kind in range(3)]
        for group in range(groups):
            at = slice((tile * groups + group) * SUB, (tile * groups + group + 1) * SUB)
            here = lane == group * (depth + 1) + depth
            packed[0] = jnp.where(here, total[at], packed[0])
            packed[1] = jnp.where(here, masked[at, 0:1], packed[1])
            packed[2] = jnp.where(here, light[at, 0:1], packed[2])
        for kind in range(3):
            out_ref[kind, rows, :] = packed[kind]


def with_rim(small, brim, depth):
    vmem = pl.BlockSpec(memory_space=pltpu.VMEM)
    return pl.pallas_call(
        functools.partial(rim_kernel, depth),
        in_specs=[vmem] * 2,
        out_specs=vmem,
        out_shape=jax.ShapeDtypeStruct(small.shape, jnp.float32),
        compiler_params=pltpu.CompilerParams(vmem_limit_bytes=4 << 20),
        cost_estimate=pl.CostEstimate(flops=10**6, bytes_accessed=10**6, transcendentals=0),
        name="rim",
    )(small, brim)


def gather_kernel(depth, lights, place_of, light_ref, parts_ref, *refs):
    count = len(refs) - 6
    chunks = refs[:count]
    image_ref, through_ref, out_ref, held, totals, sem = refs[count:]
    size, width = chunks[0].shape
    rows = (size - SUB) // depth
    for j in range(count):
        light, place = place_of(j)
        totals[place, light] = chunks[j][size - SUB :, :]
    copies = []
    for j in range(count):
        light, place = place_of(j)
        before = jnp.zeros((SUB, width), jnp.float32)
        for other in range(lights - 1):
            before = before + jnp.where(other < light, totals[place, other], 0.0)
        factor = light_ref[place] * jnp.exp(-before)
        for b in range(depth):
            for group in range(rows // SUB):
                at = b * rows + group * SUB
                lane = group * (depth + 1) + b
                held[j, b, group * SUB : (group + 1) * SUB, :] = chunks[j][at : at + SUB, :] * factor[:, lane : lane + 1]
        copy = pltpu.make_async_copy(
            held.at[j],
            out_ref.at[pl.ds(place * depth, depth), :, pl.ds(pl.multiple_of(light * width, width), width)],
            sem.at[j],
        )
        copy.start()
        copies.append(copy)
    image = jnp.zeros(image_ref.shape, jnp.float32)
    ahead = jnp.zeros(image_ref.shape, jnp.float32)
    for slab in range(parts_ref.shape[0]):
        image = image + jnp.exp(-ahead) * parts_ref[slab, 0]
        ahead = ahead + parts_ref[slab, 1]
    image_ref[...] = image
    through_ref[...] = jnp.exp(-ahead)
    for copy in copies:
        copy.wait()


def gather_block(chunks, parts, incoming, place_of, depth, lights, per):
    size, width = chunks[0].shape
    rows = (size - SUB) // depth
    return pl.pallas_call(
        functools.partial(gather_kernel, depth, lights, place_of),
        in_specs=[pl.BlockSpec(memory_space=pltpu.VMEM)] * (2 + len(chunks)),
        out_specs=[pl.BlockSpec(memory_space=pltpu.VMEM)] * 2 + [pl.BlockSpec(memory_space=pl.ANY)],
        out_shape=[jax.ShapeDtypeStruct((rows, width), jnp.float32)] * 2
        + [jax.ShapeDtypeStruct((per * depth, rows, lights * width), jnp.float32)],
        scratch_shapes=[
            pltpu.VMEM((len(chunks), depth, rows, width), jnp.float32),
            pltpu.VMEM((per, lights, SUB, width), jnp.float32),
            pltpu.SemaphoreType.DMA((len(chunks),)),
        ],
        compiler_params=pltpu.CompilerParams(vmem_limit_bytes=24 << 20),
        name="gather_block",
    )(incoming, parts, *chunks)


BAND = 32


def march_kernel(lights, occ_any, frac_ref, density_ref, albedo_ref, light_any, brim_ref, small_ref, *refs):
    arriving = refs[: lights - 1]
    phase_ref, out_ref = refs[lights - 1 : lights + 1]
    state_ref, depth_ref, brick, mask, columns, edges, weights, front, tri, field = refs[lights + 1 : lights + 11]
    density, albedo, occ_ref, light_ref, others, sem = refs[lights + 11 :]
    depth, width_a, width = density.shape
    steps = light_ref.shape[1]

    def fetches(b):
        return (
            pltpu.make_async_copy(density_ref.at[b], density.at[b], sem.at[0, b]),
            pltpu.make_async_copy(albedo_ref.at[b], albedo.at[b], sem.at[1, b]),
        )

    early = [pltpu.make_async_copy(occ_any, occ_ref, sem.at[2, 0]), pltpu.make_async_copy(light_any, light_ref, sem.at[2, 1])]
    early += [pltpu.make_async_copy(ref, others.at[i], sem.at[2, 2 + i]) for i, ref in enumerate(arriving)]
    for copy in early:
        copy.start()
    for b in range(depth):
        for fetch in fetches(b):
            fetch.start()
    for start in range(0, width_a, BAND):
        at = slice(start, start + BAND)
        levels = phase_ref[at, :]
        picked = [jnp.zeros((BAND, width), jnp.float32)] * 3
        for level in range(frac_ref.shape[1]):
            here = levels == level
            picked = [jnp.where(here, frac_ref[axis, level], value) for axis, value in enumerate(picked)]
        depth_ref[at, :] = picked[0]
        far_w = picked[1] * picked[2]
        weights[0, at, :] = 1.0 - picked[1] - picked[2] + far_w
        weights[1, at, :] = picked[1] - far_w
        weights[2, at, :] = picked[2] - far_w
        weights[3, at, :] = far_w
    rows = lax.broadcasted_iota(jnp.int32, (2 * width, width), 0) % width
    above = rows < lax.broadcasted_iota(jnp.int32, (2 * width, width), 1)
    tri[...] = jnp.where(above | (rows == width - 1), 1.0, 0.0).astype(jnp.bfloat16)
    for copy in early:
        copy.wait()
    brick_rows(occ_ref, brick, width)
    for row in range(width_a // BRICK):
        mask[row * BRICK : (row + 1) * BRICK, :] = jnp.broadcast_to(brick[row : row + 1, :], (BRICK, width))
    light = lax.axis_index("light")
    near = jnp.zeros(small_ref.shape[1:], jnp.float32)
    next_m = jnp.zeros(small_ref.shape[1:], jnp.float32)
    next_a = jnp.zeros(small_ref.shape[1:], jnp.float32)
    for by in range(1, lights):
        other = light ^ by
        near = near + jnp.where(other < light, others[by - 1, 0], 0.0)
        next_m = next_m + jnp.where(other == light + 1, others[by - 1, 1], 0.0)
        next_a = next_a + jnp.where(other == light + 1, others[by - 1, 2], 0.0)
    far = jnp.exp(-(near + small_ref[0])) * next_a
    chunks = near.shape[0] // SUB
    groups = width_a // chunks // SUB
    lane = lax.broadcasted_iota(jnp.int32, (SUB, width), 1)
    tiles = [[], []]
    for chunk in range(chunks):
        for group in range(groups):
            at = (chunk * groups + group) * SUB
            back = (width - group * steps) % width

            def turned(x):
                tile = x[chunk * SUB : (chunk + 1) * SUB]
                return pltpu.roll(tile, back, 1) if back else tile

            incoming = jnp.concatenate([light_ref[at : at + SUB, :], jnp.ones((SUB, width - steps), jnp.float32)], axis=1)
            edges[at : at + SUB, :] = pltpu.roll(turned(next_m), width - 1, 1)
            tiles[0].append(jnp.where(lane < steps, turned(near) - jnp.log(incoming), 0.0))
            tiles[1].append(jnp.where(lane < steps, incoming * turned(far), 0.0))
    target = lax.broadcasted_iota(jnp.int32, (2 * width, width), 1)
    columns[...] = jnp.zeros_like(columns)
    for kind, shift in enumerate((width - 1, 0)):
        place = ((2 * rows + shift) % width == target) & (rows < steps)
        place = jnp.where(place, 1.0, 0.0).astype(jnp.bfloat16)
        columns[...] += jnp.dot(halves(jnp.concatenate(tiles[kind], axis=0)), place, preferred_element_type=jnp.float32)
    state_ref[...] = jnp.zeros_like(state_ref)
    front[...] = jnp.ones_like(front)
    field[:, width_a:, :] = jnp.zeros((4, SUB, width), jnp.float32)
    lane = lax.broadcasted_iota(jnp.int32, (BAND, width), 1)
    last = lane == width - 1
    zeroth = lane == 0

    def slice_of(b, behind):
        if not behind:
            for fetch in fetches(b):
                fetch.wait()
        joined = []
        for start in range(0, width_a, BAND):
            at = slice(start, start + BAND)
            masked = brim_ref[0, at, :] if behind else density[b, at, :] * mask[at, :]
            field[0, at, :] = masked
            field[2, at, :] = jnp.where(last, edges[at, :], pltpu.roll(masked, width - 1, 1))
            joined.append(halves(jnp.where(last, columns[at, :], masked)))
            edges[at, :] = pltpu.roll(edges[at, :], width - 1, 1)
        within = jnp.dot(jnp.concatenate(joined, axis=0), tri[...], preferred_element_type=jnp.float32)
        for start in range(0, width_a, BAND):
            at = slice(start, start + BAND)
            lit = (brim_ref[1, at, :] if behind else albedo[b, at, :]) * jnp.exp(-within[at])
            spot = columns[at, :]
            field[1, at, :] = lit
            field[3, at, :] = pltpu.roll(jnp.where(zeroth, spot, lit), width - 1, 1)
            columns[at, :] = pltpu.roll(spot, width - 2, 1)
        started = b > 0
        for start in range(0, width_a, BAND):
            at = slice(start, start + BAND)
            below = slice(start + 1, start + BAND + 1)
            corner = [weights[i, at, :] for i in range(4)]

            def mixed(kind):
                return (corner[0] * field[kind, at, :] + corner[1] * field[kind, below, :]) + (
                    corner[2] * field[kind + 2, at, :] + corner[3] * field[kind + 2, below, :]
                )

            mix_m = mixed(0)
            mix_s = mixed(1)
            old_m = state_ref[2, at, :]
            old_s = state_ref[3, at, :]
            depth_w = depth_ref[at, :]
            extinct = jnp.where(started, old_m + depth_w * (mix_m - old_m), 0.0)
            shaded = old_s + depth_w * (mix_s - old_s)
            total = state_ref[1, at, :] + extinct
            left = jnp.exp(-total)
            state_ref[0, at, :] = state_ref[0, at, :] + (front[at, :] - left) * shaded
            state_ref[1, at, :] = total
            front[at, :] = left
            state_ref[2, at, :] = mix_m
            state_ref[3, at, :] = mix_s

    def two_slices(pair, _):
        slice_of(2 * pair, False)
        slice_of(2 * pair + 1, False)
        return 0

    lax.fori_loop(0, depth // 2, two_slices, 0)
    slice_of(depth, True)
    rows = out_ref.shape[2]
    for chunk in range(out_ref.shape[0]):
        out_ref[chunk] = state_ref[:2, chunk * rows : (chunk + 1) * rows, :]


def march(density, albedo, light_cols, brim, occupancy, fractions, small, others, rays, screens):
    depth, width_a, width = density.shape
    vmem = pl.BlockSpec(memory_space=pltpu.VMEM)
    hbm = pl.BlockSpec(memory_space=pl.ANY)
    others = [pltpu.with_memory_space_constraint(x, pltpu.HBM) for x in others]
    plane = pltpu.VMEM((width_a, width), jnp.float32)
    return pl.pallas_call(
        functools.partial(march_kernel, len(others) + 1),
        in_specs=[hbm, pl.BlockSpec(memory_space=pltpu.SMEM), hbm, hbm, hbm, vmem, vmem] + [hbm] * len(others) + [vmem],
        out_specs=vmem,
        scratch_shapes=[
            pltpu.VMEM((4, width_a, width), jnp.float32),
            plane,
            pltpu.VMEM((occupancy.shape[2], width), jnp.float32),
            plane,
            plane,
            plane,
            pltpu.VMEM((4, width_a, width), jnp.float32),
            plane,
            pltpu.VMEM((2 * width, width), jnp.bfloat16),
            pltpu.VMEM((4, width_a + SUB, width), jnp.float32),
            pltpu.VMEM(density.shape, jnp.float32),
            pltpu.VMEM(density.shape, jnp.float32),
            pltpu.VMEM(occupancy.shape, occupancy.dtype),
            pltpu.VMEM(light_cols.shape, jnp.float32),
            pltpu.VMEM((len(others), *small.shape), jnp.float32),
            pltpu.SemaphoreType.DMA((3, max(depth, 2 + len(others)))),
        ],
        out_shape=jax.ShapeDtypeStruct((screens, 2, width_a // screens, width), jnp.float32),
        compiler_params=pltpu.CompilerParams(vmem_limit_bytes=MARCH_VMEM),
        cost_estimate=pl.CostEstimate(flops=10**8, bytes_accessed=2 * depth * width_a * width * 4, transcendentals=0),
        name="march",
    )(occupancy, fractions, density, albedo, light_cols, brim, small, *others, rays)


def shifted(value, axis, by):
    peers = lax.axis_size(axis)
    return lax.ppermute(value, axis, [(i, i + by) for i in range(peers) if 0 <= i + by < peers])


def swapped(value, axis, by):
    peers = lax.axis_size(axis)
    return lax.ppermute(value, axis, [(i, i ^ by) for i in range(peers)])


def step(density, albedo, light_in, occupancy, phase, fractions):
    depth, width_a, width = density.shape
    lights, screens = lax.axis_size("light"), lax.axis_size("screen")
    light, screen = lax.axis_index("light"), lax.axis_index("screen")
    per = screens // lights
    rows = width_a // screens
    rounds = rounds_of(lights, screens)
    pairs = [round_pairs(rnd, lights, screens) for rnd in rounds]

    def spot_of(j):
        here = lax.axis_index("light"), lax.axis_index("screen")
        return target_screen(*here, (lax.rem(j, lights), lax.div(j, lights)), lights, screens)

    def place_of(j):
        return source_of(lax.axis_index("light"), lax.axis_index("screen"), rounds[j], lights, screens)

    def send(j, chunk):
        return lax.ppermute(chunk, ("light", "screen"), pairs[j])

    count = len(rounds)
    flags = pltpu.with_memory_space_constraint(occupancy.transpose(0, 2, 1), pltpu.HBM)
    density = pltpu.with_memory_space_constraint(density, pltpu.HBM)
    albedo = pltpu.with_memory_space_constraint(albedo, pltpu.HBM)
    early = lit_chunks(density, albedo, flags, spot_of, 0, 2, screens)
    late = lit_chunks(density, albedo, flags, spot_of, 2, count - 2, screens, early[-1])
    arrived = [send(j, chunk) for j, chunk in enumerate(early[:2] + late[:-1])]
    brim = shifted(early[2], "screen", -1)
    small = with_rim(late[-1], brim, depth)
    others = [swapped(small, "light", by) for by in range(1, lights)]
    light_cols = jnp.pad(light_in, ((0, 1), (0, 0)), constant_values=1.0)
    light_cols = lax.dynamic_slice_in_dim(light_cols, screen * depth, depth + 1, 0).T
    rays = lax.dynamic_slice_in_dim(phase, light * width, width, 1)
    parts = march(density, albedo, light_cols, brim, flags, fractions, small, others, rays, screens)
    got = lax.all_to_all(parts, "screen", split_axis=0, concat_axis=0, tiled=True)
    incoming = lax.dynamic_slice(light_in, (light * per * depth, screen * rows), (per * depth, rows))
    incoming = jnp.pad(incoming.reshape(per, depth, rows // SUB, SUB), ((0, 0), (0, 1), (0, 0), (0, 0)))
    incoming = incoming.transpose(0, 3, 2, 1).reshape(per, SUB, rows // SUB * (depth + 1))
    incoming = jnp.pad(incoming, ((0, 0), (0, 0), (0, width - incoming.shape[2])))
    return gather_block(arrived, got, incoming, place_of, depth, lights, per)


def local(*args):
    return tuple(step(*args))


def solution(mesh):
    return jax.shard_map(
        local,
        mesh=mesh,
        in_specs=(
            P("screen", None, "light"),
            P("screen", None, "light"),
            P(),
            P("screen", None, "light"),
            P(),
            P(),
        ),
        out_specs=(P("screen", "light"), P("screen", "light"), P("light", "screen", None)),
        check_vma=False,
    )
```

time: 109 us -> 94.6 us (0.87)
  the two profiles are of different devices: /device:TPU:3 before, /device:TPU:27 now
where the time goes in v2:
time: 94.6 us; the launch traced here: 94.2 us
  waiting for transfers between devices  41.6 us (44%)
  starting transfers between devices  31.6 us (33%)
  Pallas kernels  17.9 us (19%)
  local copies, waits for them, and re-layouts  2.25 us (2%)
    ppermute x8, waiting for transfers between devices, send(): return lax.ppermute(chunk, ('light', 'screen'), pairs[j])  29.4 us
    ppermute x8, starting transfers between devices, send(): return lax.ppermute(chunk, ('light', 'screen'), pairs[j])  20.2 us
    ppermute x3, waiting for transfers between devices, swapped(): return lax.ppermute(value, axis, [(i, i ^ by) for i in range(peers)])  12.2 us
    pallas_call x1, Pallas kernels, march(): pl.pallas_call(functools.partial(march_kernel, len(others) + 1), in_specs...  8.57 us
    all_to_all x1, starting transfers between devices, step(): lax.all_to_all(parts, 'screen', split_axis=0, concat_axis=0, tiled=True)  7.63 us
    pallas_call x2, Pallas kernels, lit_chunks(): pl.pallas_call(functools.partial(chunk_kernel, count, spot_of, first), in...  6.69 us
    ppermute x1, starting transfers between devices, shifted(): lax.ppermute(value, axis, [(i, i + by) for i in range(peers) if 0 <= i +...  2.6 us
    pallas_call x1, Pallas kernels, gather_block(): pl.pallas_call(functools.partial(gather_kernel, depth, lights, place_of),...  2.44 us
  transfers between devices with their start and end apart: 13, of which 7 were waited for; matrix products, arithmetic and copies ran while one was open for 1% of the time, Pallas kernels for 14%

profile of v2, /device:TPU:27, one launch (start us, length us, event | category | flops | bytes accessed | tf_op | source)
XLA Modules:
  0.0 94.2 jit_solution(2183223711607925271)
XLA Ops:
  0.6 0.0 copy-start
  0.6 2.2 %lit_chunks.2 = (f32[520,128]{1,0:T(8,128)S(1)}, f32[520,128]{1,0:T(8,128)S(1)}, f32[2,256,128]{2,1,0:T(8,128)S(1)}, f32[3,16,128]{2,1,0:T(8,128)S(1)}) custom-call(s32[1,8,16]{2,1,0:T(8,128)} %bitcast.7, f32[16,256,128]{2,1,0:T(8,128)} %density_ref.1, f32[16,256,128]{2,1,0:T(8,128)} %albedo_ref.1), custom_call_target="tpu_custom_call" | custom-call | flops 20000000 | bytes 1597440 | tf_op jit(solution)/shard_map/lit_chunks/pallas_call | solution.py:146
  2.8 2.6 %collective-permute-start = (f32[2,256,128]{2,1,0:T(8,128)S(1)}, f32[2,256,128]{2,1,0:T(8,128)S(1)}, u32[]{:S(2)}, u32[]{:S(2)}) collective-permute-start(f32[2,256,128]{2,1,0:T(8,128)S(1)} %get-tuple-element.14), channel_id=1, source_target_pairs={{1,0},{2,1},{3,2},{4,3},{5,4},{6,5},{7,6},{9,8},{10,9},{11,10},{12... | collective-permute-start | bytes 786440 | tf_op jit(solution)/shard_map/ppermute | solution.py:443
  5.4 3.0 %collective-permute-start.4 = (f32[520,128]{1,0:T(8,128)S(1)}, f32[520,128]{1,0:T(8,128)S(1)}, u32[]{:S(2)}, u32[]{:S(2)}) collective-permute-start(f32[520,128]{1,0:T(8,128)S(1)} %get-tuple-element.17), channel_id=1, source_target_pairs={{0,0},{1,1},{2,12},{3,13},{4,18},{5,19},{6,30},{7,31},{8,2},{9,3},... | collective-permute-start | bytes 798728 | tf_op jit(solution)/shard_map/ppermute | solution.py:468
  8.4 2.0 %collective-permute-start.5 = (f32[520,128]{1,0:T(8,128)S(1)}, f32[520,128]{1,0:T(8,128)S(1)}, u32[]{:S(2)}, u32[]{:S(2)}) collective-permute-start(f32[520,128]{1,0:T(8,128)S(1)} %get-tuple-element.18), channel_id=1, source_target_pairs={{0,2},{1,3},{2,14},{3,15},{4,16},{5,17},{6,28},{7,29},{8,0},{9,1},... | collective-permute-start | bytes 798728 | tf_op jit(solution)/shard_map/ppermute | solution.py:468
  10.5 0.0 copy-start.2
  10.5 4.5 %lit_chunks.3 = (f32[520,128]{1,0:T(8,128)S(1)}, f32[520,128]{1,0:T(8,128)}, f32[520,128]{1,0:T(8,128)}, f32[520,128]{1,0:T(8,128)}, f32[520,128]{1,0:T(8,128)S(...) custom-call(s32[1,8,16]{2,1,0:T(8,128)} %bitcast.8, f32[16,256,128]{2,1,0:T(8,128)} %density_ref.1, ...), custom_call_target="tpu_custom_call" | custom-call | flops 60000000 | bytes 4792320 | tf_op jit(solution)/shard_map/lit_chunks/pallas_call | solution.py:146
  15.1 4.9 %collective-permute-start.6 = (f32[520,128]{1,0:T(8,128)S(1)}, f32[520,128]{1,0:T(8,128)S(1)}, u32[]{:S(2)}, u32[]{:S(2)}) collective-permute-start(f32[520,128]{1,0:T(8,128)S(1)} %get-tuple-element.19), channel_id=1, source_target_pairs={{0,4},{1,5},{2,8},{3,9},{4,22},{5,23},{6,26},{7,27},{8,6},{9,7},{1... | collective-permute-start | bytes 798728 | tf_op jit(solution)/shard_map/ppermute | solution.py:468
  20.0 0.1 copy.12
  20.1 0.2 rim.1.small_ref
  20.3 1.2 %collective-permute-start.3 = (f32[3,64,128]{2,1,0:T(8,128)S(1)}, f32[3,64,128]{2,1,0:T(8,128)S(1)}, u32[]{:S(2)}, u32[]{:S(2)}) collective-permute-start(f32[3,64,128]{2,1,0:T(8,128)S(1)} %rim.1.small_ref), channel_id=1, source_target_pairs={{0,24},{8,16},{16,8},{24,0},{1,25},{9,17},{17,9},{25,1},{2,26},{10... | collective-permute-start | bytes 294920 | tf_op jit(solution)/shard_map/ppermute | solution.py:448
  21.4 0.1 collective-permute-start.2
  21.5 8.7 %collective-permute-done.3.refs_2_ = f32[3,64,128]{2,1,0:T(8,128)S(1)} collective-permute-done((f32[3,64,128]{2,1,0:T(8,128)S(1)}, f32[3,64,128]{2,1,0:T(8,128)S(1)}, u32[]{:S(2)}, u32[]{:S(2)}) %collective-permute-start.3) | collective-permute-done | bytes 98336 | tf_op jit(solution)/shard_map/ppermute | solution.py:448
  30.3 0.1 fusion.light_any
  30.4 3.2 %collective-permute-done.2.refs_1_ = f32[3,64,128]{2,1,0:T(8,128)S(1)} collective-permute-done((f32[3,64,128]{2,1,0:T(8,128)S(1)}, f32[3,64,128]{2,1,0:T(8,128)S(1)}, u32[]{:S(2)}, u32[]{:S(2)}) %collective-permute-start.2) | collective-permute-done | bytes 98336 | tf_op jit(solution)/shard_map/ppermute | solution.py:448
  33.5 0.3 collective-permute-done.1.refs_0_
  33.9 0.3 copy-done.4
  34.2 0.6 copy-done.5
  34.8 8.6 %march.1 = f32[8,2,32,128]{3,2,1,0:T(8,128)} custom-call(s32[1,8,16]{2,1,0:T(8,128)} %bitcast.9, f32[3,16]{1,0:T(4,128)S(1)} %copy-done.1, f32[16,256,128]{2,1,0:T(8,128)} %density_ref.1, f32[16,256,128]{2,1,0:T(8,128)} %albedo_ref.1, f32[256,17]{1,0:T(8,128)S(1)} %fusion.light_any, f32[2,256,128]{2,1,0:T(8,128)S(1)} %collective-permute-done.brim_ref, ...), custom_call_target="tpu_custom_call" | custom-call | flops 100000000 | bytes 4194304 | tf_op jit(solution)/shard_map/march/pallas_call | solution.py:412
  43.4 7.6 %all-to-all-start = ((f32[8,2,32,128]{3,2,1,0:T(8,128)}), f32[8,2,32,128]{3,2,1,0:T(8,128)S(1)}, u32[]{:S(2)}, u32[]{:S(2)}) async-start(f32[8,2,32,128]{3,2,1,0:T(8,128)} %march.1), calls=%async_computation | async-start | bytes 524288 | tf_op jit(solution)/shard_map/all_to_all | solution.py:484
  51.0 2.1 %collective-permute-start.7 = (f32[520,128]{1,0:T(8,128)}, f32[520,128]{1,0:T(8,128)S(1)}, u32[]{:S(2)}, u32[]{:S(2)}) collective-permute-start(f32[520,128]{1,0:T(8,128)} %get-tuple-element.20), channel_id=1, source_target_pairs={{0,6},{1,7},{2,10},{3,11},{4,20},{5,21},{6,24},{7,25},{8,4},{9,5},... | collective-permute-start | bytes 798728 | tf_op jit(solution)/shard_map/ppermute | solution.py:468
  53.1 2.1 %collective-permute-start.8 = (f32[520,128]{1,0:T(8,128)}, f32[520,128]{1,0:T(8,128)S(1)}, u32[]{:S(2)}, u32[]{:S(2)}) collective-permute-start(f32[520,128]{1,0:T(8,128)} %get-tuple-element.21), channel_id=1, source_target_pairs={{0,1},{1,0},{2,13},{3,12},{4,19},{5,18},{6,31},{7,30},{8,3},{9,2},... | collective-permute-start | bytes 798728 | tf_op jit(solution)/shard_map/ppermute | solution.py:468
  55.2 6.1 %collective-permute-start.10 = (f32[520,128]{1,0:T(8,128)S(1)}, f32[520,128]{1,0:T(8,128)S(1)}, u32[]{:S(2)}, u32[]{:S(2)}) collective-permute-start(f32[520,128]{1,0:T(8,128)S(1)} %get-tuple-element.23), channel_id=1, source_target_pairs={{0,5},{1,4},{2,9},{3,8},{4,23},{5,22},{6,27},{7,26},{8,7},{9,6},{1... | collective-permute-start | bytes 798728 | tf_op jit(solution)/shard_map/ppermute | solution.py:468
  61.2 0.8 dynamic_slice.9
  62.0 0.1 copy.10
  62.1 0.1 reshape.12
  62.3 0.1 reshape.13
  62.3 7.5 %collective-permute-done.7.refs_3_ = f32[520,128]{1,0:T(8,128)S(1)} collective-permute-done((f32[520,128]{1,0:T(8,128)}, f32[520,128]{1,0:T(8,128)S(1)}, u32[]{:S(2)}, u32[]{:S(2)}) %collective-permute-start.7) | collective-permute-done | bytes 266272 | tf_op jit(solution)/shard_map/ppermute | solution.py:468
  69.9 11.1 %collective-permute-done.8.refs_4_ = f32[520,128]{1,0:T(8,128)S(1)} collective-permute-done((f32[520,128]{1,0:T(8,128)}, f32[520,128]{1,0:T(8,128)S(1)}, u32[]{:S(2)}, u32[]{:S(2)}) %collective-permute-start.8) | collective-permute-done | bytes 266272 | tf_op jit(solution)/shard_map/ppermute | solution.py:468
  81.0 7.0 %collective-permute-done.9.refs_5_ = f32[520,128]{1,0:T(8,128)S(1)} collective-permute-done((f32[520,128]{1,0:T(8,128)}, f32[520,128]{1,0:T(8,128)S(1)}, u32[]{:S(2)}, u32[]{:S(2)}) %collective-permute-start.9) | collective-permute-done | bytes 266272 | tf_op jit(solution)/shard_map/ppermute | solution.py:468
  88.0 3.7 %collective-permute-done.11.refs_7_ = f32[520,128]{1,0:T(8,128)S(1)} collective-permute-done((f32[520,128]{1,0:T(8,128)S(1)}, f32[520,128]{1,0:T(8,128)S(1)}, u32[]{:S(2)}, u32[]{:S(2)}) %collective-permute-start.11) | collective-permute-done | bytes 266272 | tf_op jit(solution)/shard_map/ppermute | solution.py:468
  91.7 2.4 %gather_block.1 = (f32[32,128]{1,0:T(8,128)}, f32[32,128]{1,0:T(8,128)}, f32[32,32,512]{2,1,0:T(8,128)}) custom-call(f32[2,8,128]{2,1,0:T(8,128)S(1)} %pad.13.light_ref, f32[8,2,32,128]{3,2,1,0:T(8,128)S(1)} %all-to-all-done.parts_ref, f32[520,128]{1,0:T(8,128)S(1)} %collective-permute-done.4.refs_0_, f32[520,128]{1,0:T(8,128)S(1)} %collective-permute-done.5.refs_1_, ...), custom_call_target="tpu_custom_call" | custom-call | tf_op jit(solution)/shard_map/gather_block/pallas_call | solution.py:247
  (21 shorter events, 0.1 us)
Async XLA Ops:
  0.6 20.8 %copy-start = (s32[256,512]{1,0:T(8,128)S(1)}, s32[256,512]{1,0:T(8,128)}, u32[]{:S(2)}) copy-start(s32[256,512]{1,0:T(8,128)} %param.10) | copy-start | bytes 1572868
  2.8 17.3 %collective-permute-start = (f32[2,256,128]{2,1,0:T(8,128)S(1)}, f32[2,256,128]{2,1,0:T(8,128)S(1)}, u32[]{:S(2)}, u32[]{:S(2)}) collective-permute-start(f32[2,256,128]{2,1,0:T(8,128)S(1)} %get-tuple-element.14), channel_id=1, source_target_pairs={{1,0},{2,1},{3,2},{4,3},{5,4},{6,5},{7,6},{9,8},{10,9},{11,10},{12... | collective-permute-start | bytes 786440 | tf_op jit(solution)/shard_map/ppermute | solution.py:443
  5.4 49.7 %collective-permute-start.4 = (f32[520,128]{1,0:T(8,128)S(1)}, f32[520,128]{1,0:T(8,128)S(1)}, u32[]{:S(2)}, u32[]{:S(2)}) collective-permute-start(f32[520,128]{1,0:T(8,128)S(1)} %get-tuple-element.17), channel_id=1, source_target_pairs={{0,0},{1,1},{2,12},{3,13},{4,18},{5,19},{6,30},{7,31},{8,2},{9,3},... | collective-permute-start | bytes 798728 | tf_op jit(solution)/shard_map/ppermute | solution.py:468
  8.4 46.7 %collective-permute-start.5 = (f32[520,128]{1,0:T(8,128)S(1)}, f32[520,128]{1,0:T(8,128)S(1)}, u32[]{:S(2)}, u32[]{:S(2)}) collective-permute-start(f32[520,128]{1,0:T(8,128)S(1)} %get-tuple-element.18), channel_id=1, source_target_pairs={{0,2},{1,3},{2,14},{3,15},{4,16},{5,17},{6,28},{7,29},{8,0},{9,1},... | collective-permute-start | bytes 798728 | tf_op jit(solution)/shard_map/ppermute | solution.py:468
  10.5 9.5 %copy-start.2 = (f32[128,256]{1,0:T(8,128)S(1)}, f32[128,256]{1,0:T(8,128)}, u32[]{:S(2)}) copy-start(f32[128,256]{1,0:T(8,128)} %param.8) | copy-start | bytes 393220
  10.5 24.3 %copy-start.1 = (f32[3,16]{1,0:T(4,128)S(1)}, f32[3,16]{1,0:T(4,128)}, u32[]{:S(2)}) copy-start(f32[3,16]{1,0:T(4,128)} %frac_ref.1) | copy-start | bytes 580
  15.1 46.2 %collective-permute-start.6 = (f32[520,128]{1,0:T(8,128)S(1)}, f32[520,128]{1,0:T(8,128)S(1)}, u32[]{:S(2)}, u32[]{:S(2)}) collective-permute-start(f32[520,128]{1,0:T(8,128)S(1)} %get-tuple-element.19), channel_id=1, source_target_pairs={{0,4},{1,5},{2,8},{3,9},{4,22},{5,23},{6,26},{7,27},{8,6},{9,7},{1... | collective-permute-start | bytes 798728 | tf_op jit(solution)/shard_map/ppermute | solution.py:468
  20.3 10.0 %collective-permute-start.3 = (f32[3,64,128]{2,1,0:T(8,128)S(1)}, f32[3,64,128]{2,1,0:T(8,128)S(1)}, u32[]{:S(2)}, u32[]{:S(2)}) collective-permute-start(f32[3,64,128]{2,1,0:T(8,128)S(1)} %rim.1.small_ref), channel_id=1, source_target_pairs={{0,24},{8,16},{16,8},{24,0},{1,25},{9,17},{17,9},{25,1},{2,26},{10... | collective-permute-start | bytes 294920 | tf_op jit(solution)/shard_map/ppermute | solution.py:448
  21.4 12.1 %collective-permute-start.2 = (f32[3,64,128]{2,1,0:T(8,128)S(1)}, f32[3,64,128]{2,1,0:T(8,128)S(1)}, u32[]{:S(2)}, u32[]{:S(2)}) collective-permute-start(f32[3,64,128]{2,1,0:T(8,128)S(1)} %rim.1.small_ref), channel_id=1, source_target_pairs={{0,16},{8,24},{16,0},{24,8},{1,17},{9,25},{17,1},{25,9},{2,18},{10... | collective-permute-start | bytes 294920 | tf_op jit(solution)/shard_map/ppermute | solution.py:448
  30.2 3.6 %copy-start.3 = (f32[3,64,128]{2,1,0:T(8,128)}, f32[3,64,128]{2,1,0:T(8,128)S(1)}, u32[]{:S(2)}) copy-start(f32[3,64,128]{2,1,0:T(8,128)S(1)} %collective-permute-done.3.refs_2_) | copy-start | bytes 294916
  30.3 3.6 %collective-permute-start.1 = (f32[3,64,128]{2,1,0:T(8,128)S(1)}, f32[3,64,128]{2,1,0:T(8,128)S(1)}, u32[]{:S(2)}, u32[]{:S(2)}) collective-permute-start(f32[3,64,128]{2,1,0:T(8,128)S(1)} %rim.1.small_ref), channel_id=1, source_target_pairs={{0,8},{8,0},{16,24},{24,16},{1,9},{9,1},{17,25},{25,17},{2,10},{10... | collective-permute-start | bytes 294920 | tf_op jit(solution)/shard_map/ppermute | solution.py:448
  33.5 0.6 copy-start.4
  34.2 0.6 copy-start.5
  43.4 48.3 %all-to-all-start = ((f32[8,2,32,128]{3,2,1,0:T(8,128)}), f32[8,2,32,128]{3,2,1,0:T(8,128)S(1)}, u32[]{:S(2)}, u32[]{:S(2)}) async-start(f32[8,2,32,128]{3,2,1,0:T(8,128)} %march.1), calls=%async_computation | async-start | bytes 524288 | tf_op jit(solution)/shard_map/all_to_all | solution.py:484
  51.0 18.9 %collective-permute-start.7 = (f32[520,128]{1,0:T(8,128)}, f32[520,128]{1,0:T(8,128)S(1)}, u32[]{:S(2)}, u32[]{:S(2)}) collective-permute-start(f32[520,128]{1,0:T(8,128)} %get-tuple-element.20), channel_id=1, source_target_pairs={{0,6},{1,7},{2,10},{3,11},{4,20},{5,21},{6,24},{7,25},{8,4},{9,5},... | collective-permute-start | bytes 798728 | tf_op jit(solution)/shard_map/ppermute | solution.py:468
  53.1 27.9 %collective-permute-start.8 = (f32[520,128]{1,0:T(8,128)}, f32[520,128]{1,0:T(8,128)S(1)}, u32[]{:S(2)}, u32[]{:S(2)}) collective-permute-start(f32[520,128]{1,0:T(8,128)} %get-tuple-element.21), channel_id=1, source_target_pairs={{0,1},{1,0},{2,13},{3,12},{4,19},{5,18},{6,31},{7,30},{8,3},{9,2},... | collective-permute-start | bytes 798728 | tf_op jit(solution)/shard_map/ppermute | solution.py:468
  55.2 32.9 %collective-permute-start.9 = (f32[520,128]{1,0:T(8,128)}, f32[520,128]{1,0:T(8,128)S(1)}, u32[]{:S(2)}, u32[]{:S(2)}) collective-permute-start(f32[520,128]{1,0:T(8,128)} %get-tuple-element.22), channel_id=1, source_target_pairs={{0,3},{1,2},{2,15},{3,14},{4,17},{5,16},{6,29},{7,28},{8,1},{9,0},... | collective-permute-start | bytes 798728 | tf_op jit(solution)/shard_map/ppermute | solution.py:468
  55.2 32.9 %collective-permute-start.10 = (f32[520,128]{1,0:T(8,128)S(1)}, f32[520,128]{1,0:T(8,128)S(1)}, u32[]{:S(2)}, u32[]{:S(2)}) collective-permute-start(f32[520,128]{1,0:T(8,128)S(1)} %get-tuple-element.23), channel_id=1, source_target_pairs={{0,5},{1,4},{2,9},{3,8},{4,23},{5,22},{6,27},{7,26},{8,7},{9,6},{1... | collective-permute-start | bytes 798728 | tf_op jit(solution)/shard_map/ppermute | solution.py:468
  61.2 30.5 %collective-permute-start.11 = (f32[520,128]{1,0:T(8,128)S(1)}, f32[520,128]{1,0:T(8,128)S(1)}, u32[]{:S(2)}, u32[]{:S(2)}) collective-permute-start(f32[520,128]{1,0:T(8,128)S(1)} %get-tuple-element.24), channel_id=1, source_target_pairs={{0,7},{1,6},{2,11},{3,10},{4,21},{5,20},{6,25},{7,24},{8,5},{9,4},... | collective-permute-start | bytes 798728 | tf_op jit(solution)/shard_map/ppermute | solution.py:468

commit v3 on v2

--- a/solution.py
+++ b/solution.py
@@ -471,10 +471,10 @@
     flags = pltpu.with_memory_space_constraint(occupancy.transpose(0, 2, 1), pltpu.HBM)
     density = pltpu.with_memory_space_constraint(density, pltpu.HBM)
     albedo = pltpu.with_memory_space_constraint(albedo, pltpu.HBM)
-    early = lit_chunks(density, albedo, flags, spot_of, 0, 2, screens)
-    late = lit_chunks(density, albedo, flags, spot_of, 2, count - 2, screens, early[-1])
-    arrived = [send(j, chunk) for j, chunk in enumerate(early[:2] + late[:-1])]
-    brim = shifted(early[2], "screen", -1)
+    early = lit_chunks(density, albedo, flags, spot_of, 0, 3, screens)
+    late = lit_chunks(density, albedo, flags, spot_of, 3, count - 3, screens, early[-1])
+    arrived = [send(j, chunk) for j, chunk in enumerate(early[:3] + late[:-1])]
+    brim = shifted(early[3], "screen", -1)
     small = with_rim(late[-1], brim, depth)
     others = [swapped(small, "light", by) for by in range(1, lights)]
     light_cols = jnp.pad(light_in, ((0, 1), (0, 0)), constant_values=1.0)

time: 94.6 us -> 91.8 us (0.970)
  waiting for transfers between devices: 41.6 us -> 38.1 us
    ppermute x3, waiting for transfers between devices: 12.2 us -> 9.58 us  [swapped(): return lax.ppermute(value, axis, [(i, i ^ by) for i in range(peers)])]
    ppermute x3, starting transfers between devices: 1.23 us -> 3.72 us  [swapped(): return lax.ppermute(value, axis, [(i, i ^ by) for i in range(peers)])]
    all_to_all x1, starting transfers between devices: 7.63 us -> 5.38 us  [step(): lax.all_to_all(parts, 'screen', split_axis=0, concat_axis=0, tiled=True)]
  transfers between devices with their start and end apart: 13 -> 13, of which waited for: 7 -> 6; matrix products, arithmetic and copies ran while one was open for 1% -> 1% of each run, Pallas kernels for 14% -> 14%
where the time goes in v3:
time: 91.8 us; the launch traced here: 91.3 us
  waiting for transfers between devices  38.1 us (42%)
  starting transfers between devices  31.9 us (35%)
  Pallas kernels  18 us (20%)
  local copies, waits for them, and re-layouts  2.55 us (3%)
    ppermute x8, waiting for transfers between devices, send(): return lax.ppermute(chunk, ('light', 'screen'), pairs[j])  28.5 us
    ppermute x8, starting transfers between devices, send(): return lax.ppermute(chunk, ('light', 'screen'), pairs[j])  20.2 us
    ppermute x3, waiting for transfers between devices, swapped(): return lax.ppermute(value, axis, [(i, i ^ by) for i in range(peers)])  9.58 us
    pallas_call x1, Pallas kernels, march(): pl.pallas_call(functools.partial(march_kernel, len(others) + 1), in_specs...  8.76 us
    pallas_call x2, Pallas kernels, lit_chunks(): pl.pallas_call(functools.partial(chunk_kernel, count, spot_of, first), in...  6.64 us
    all_to_all x1, starting transfers between devices, step(): lax.all_to_all(parts, 'screen', split_axis=0, concat_axis=0, tiled=True)  5.38 us
    ppermute x3, starting transfers between devices, swapped(): return lax.ppermute(value, axis, [(i, i ^ by) for i in range(peers)])  3.72 us
    ppermute x1, starting transfers between devices, shifted(): lax.ppermute(value, axis, [(i, i + by) for i in range(peers) if 0 <= i +...  2.59 us
  transfers between devices with their start and end apart: 13, of which 6 were waited for; matrix products, arithmetic and copies ran while one was open for 1% of the time, Pallas kernels for 14%

profile of v3, /device:TPU:27, one launch (start us, length us, event | category | flops | bytes accessed | tf_op | source)
XLA Modules:
  0.0 91.3 jit_solution(6155416144854441477)
XLA Ops:
  0.6 0.0 copy-start
  0.7 2.7 %lit_chunks.2 = (f32[520,128]{1,0:T(8,128)S(1)}, f32[520,128]{1,0:T(8,128)S(1)}, f32[520,128]{1,0:T(8,128)S(1)}, f32[2,256,128]{2,1,0:T(8,128)S(1)}, f32[3,24,128]{2,1,0:T(8,128)S(1)}) custom-call(s32[1,8,16]{2,1,0:T(8,128)} %bitcast.7, f32[16,256,128]{2,1,0:T(8,128)} %density_ref.1, f32[16,256,128]{2,1,0:T(8,128)} %albedo_ref.1), custom_call_target="tpu_custom_call" | custom-call | flops 30000000 | bytes 2396160 | tf_op jit(solution)/shard_map/lit_chunks/pallas_call | solution.py:146
  3.3 2.6 %collective-permute-start = (f32[2,256,128]{2,1,0:T(8,128)S(1)}, f32[2,256,128]{2,1,0:T(8,128)S(1)}, u32[]{:S(2)}, u32[]{:S(2)}) collective-permute-start(f32[2,256,128]{2,1,0:T(8,128)S(1)} %get-tuple-element.14), channel_id=1, source_target_pairs={{1,0},{2,1},{3,2},{4,3},{5,4},{6,5},{7,6},{9,8},{10,9},{11,10},{12... | collective-permute-start | bytes 786440 | tf_op jit(solution)/shard_map/ppermute | solution.py:443
  5.9 3.0 %collective-permute-start.4 = (f32[520,128]{1,0:T(8,128)S(1)}, f32[520,128]{1,0:T(8,128)S(1)}, u32[]{:S(2)}, u32[]{:S(2)}) collective-permute-start(f32[520,128]{1,0:T(8,128)S(1)} %get-tuple-element.17), channel_id=1, source_target_pairs={{0,0},{1,1},{2,12},{3,13},{4,18},{5,19},{6,30},{7,31},{8,2},{9,3},... | collective-permute-start | bytes 798728 | tf_op jit(solution)/shard_map/ppermute | solution.py:468
  9.0 2.0 %collective-permute-start.5 = (f32[520,128]{1,0:T(8,128)S(1)}, f32[520,128]{1,0:T(8,128)S(1)}, u32[]{:S(2)}, u32[]{:S(2)}) collective-permute-start(f32[520,128]{1,0:T(8,128)S(1)} %get-tuple-element.18), channel_id=1, source_target_pairs={{0,2},{1,3},{2,14},{3,15},{4,16},{5,17},{6,28},{7,29},{8,0},{9,1},... | collective-permute-start | bytes 798728 | tf_op jit(solution)/shard_map/ppermute | solution.py:468
  11.0 4.9 %collective-permute-start.6 = (f32[520,128]{1,0:T(8,128)S(1)}, f32[520,128]{1,0:T(8,128)S(1)}, u32[]{:S(2)}, u32[]{:S(2)}) collective-permute-start(f32[520,128]{1,0:T(8,128)S(1)} %get-tuple-element.19), channel_id=1, source_target_pairs={{0,4},{1,5},{2,8},{3,9},{4,22},{5,23},{6,26},{7,27},{8,6},{9,7},{1... | collective-permute-start | bytes 798728 | tf_op jit(solution)/shard_map/ppermute | solution.py:468
  15.9 0.1 copy.12
  16.0 4.0 %lit_chunks.3 = (f32[520,128]{1,0:T(8,128)}, f32[520,128]{1,0:T(8,128)}, f32[520,128]{1,0:T(8,128)}, f32[520,128]{1,0:T(8,128)S(1)}, f32[520,128]{1,0:T(8,128)S(1)}, /*index=5*/f32[3,64,128]{2,1,0:T(8,128)S(1)}) custom-call(s32[1,8,16]{2,1,0:T(8,128)} %bitcast.8, f32[16,256,128]{2,1,0:T(8,128)} %density_ref.1, f32[16,256,128]{2,1,0:T(8,128)} %albedo_ref.1, ...), custom_call_target="tpu_custom_call" | custom-call | flops 50000000 | bytes 3993600 | tf_op jit(solution)/shard_map/lit_chunks/pallas_call | solution.py:146
  20.0 0.2 rim.1.small_ref
  20.2 1.2 %collective-permute-start.3 = (f32[3,64,128]{2,1,0:T(8,128)S(1)}, f32[3,64,128]{2,1,0:T(8,128)S(1)}, u32[]{:S(2)}, u32[]{:S(2)}) collective-permute-start(f32[3,64,128]{2,1,0:T(8,128)S(1)} %rim.1.small_ref), channel_id=1, source_target_pairs={{0,24},{8,16},{16,8},{24,0},{1,25},{9,17},{17,9},{25,1},{2,26},{10... | collective-permute-start | bytes 294920 | tf_op jit(solution)/shard_map/ppermute | solution.py:448
  21.4 0.1 collective-permute-start.2
  21.5 4.6 %collective-permute-done.3.refs_2_ = f32[3,64,128]{2,1,0:T(8,128)S(1)} collective-permute-done((f32[3,64,128]{2,1,0:T(8,128)S(1)}, f32[3,64,128]{2,1,0:T(8,128)S(1)}, u32[]{:S(2)}, u32[]{:S(2)}) %collective-permute-start.3) | collective-permute-done | bytes 98336 | tf_op jit(solution)/shard_map/ppermute | solution.py:448
  26.1 2.5 %collective-permute-start.1 = (f32[3,64,128]{2,1,0:T(8,128)S(1)}, f32[3,64,128]{2,1,0:T(8,128)S(1)}, u32[]{:S(2)}, u32[]{:S(2)}) collective-permute-start(f32[3,64,128]{2,1,0:T(8,128)S(1)} %rim.1.small_ref), channel_id=1, source_target_pairs={{0,8},{8,0},{16,24},{24,16},{1,9},{9,1},{17,25},{25,17},{2,10},{10... | collective-permute-start | bytes 294920 | tf_op jit(solution)/shard_map/ppermute | solution.py:448
  28.6 0.1 fusion.light_any
  28.7 5.0 %collective-permute-done.2.refs_1_ = f32[3,64,128]{2,1,0:T(8,128)S(1)} collective-permute-done((f32[3,64,128]{2,1,0:T(8,128)S(1)}, f32[3,64,128]{2,1,0:T(8,128)S(1)}, u32[]{:S(2)}, u32[]{:S(2)}) %collective-permute-start.2) | collective-permute-done | bytes 98336 | tf_op jit(solution)/shard_map/ppermute | solution.py:448
  33.7 0.6 copy-done.4
  34.3 0.6 copy-done.5
  34.9 8.8 %march.1 = f32[8,2,32,128]{3,2,1,0:T(8,128)} custom-call(s32[1,8,16]{2,1,0:T(8,128)} %bitcast.9, f32[3,16]{1,0:T(4,128)S(1)} %copy-done.1, f32[16,256,128]{2,1,0:T(8,128)} %density_ref.1, f32[16,256,128]{2,1,0:T(8,128)} %albedo_ref.1, f32[256,17]{1,0:T(8,128)S(1)} %fusion.light_any, f32[2,256,128]{2,1,0:T(8,128)S(1)} %collective-permute-done.brim_ref, ...), custom_call_target="tpu_custom_call" | custom-call | flops 100000000 | bytes 4194304 | tf_op jit(solution)/shard_map/march/pallas_call | solution.py:412
  43.7 5.4 %all-to-all-start = ((f32[8,2,32,128]{3,2,1,0:T(8,128)}), f32[8,2,32,128]{3,2,1,0:T(8,128)S(1)}, u32[]{:S(2)}, u32[]{:S(2)}) async-start(f32[8,2,32,128]{3,2,1,0:T(8,128)} %march.1), calls=%async_computation | async-start | bytes 524288 | tf_op jit(solution)/shard_map/all_to_all | solution.py:484
  49.1 3.1 %collective-permute-start.7 = (f32[520,128]{1,0:T(8,128)}, f32[520,128]{1,0:T(8,128)S(1)}, u32[]{:S(2)}, u32[]{:S(2)}) collective-permute-start(f32[520,128]{1,0:T(8,128)} %get-tuple-element.20), channel_id=1, source_target_pairs={{0,6},{1,7},{2,10},{3,11},{4,20},{5,21},{6,24},{7,25},{8,4},{9,5},... | collective-permute-start | bytes 798728 | tf_op jit(solution)/shard_map/ppermute | solution.py:468
  52.2 0.6 collective-permute-start.8
  52.8 1.5 %collective-permute-start.9 = (f32[520,128]{1,0:T(8,128)}, f32[520,128]{1,0:T(8,128)S(1)}, u32[]{:S(2)}, u32[]{:S(2)}) collective-permute-start(f32[520,128]{1,0:T(8,128)} %get-tuple-element.22), channel_id=1, source_target_pairs={{0,3},{1,2},{2,15},{3,14},{4,17},{5,16},{6,29},{7,28},{8,1},{9,0},... | collective-permute-start | bytes 798728 | tf_op jit(solution)/shard_map/ppermute | solution.py:468
  54.3 5.0 %collective-permute-start.10 = (f32[520,128]{1,0:T(8,128)S(1)}, f32[520,128]{1,0:T(8,128)S(1)}, u32[]{:S(2)}, u32[]{:S(2)}) collective-permute-start(f32[520,128]{1,0:T(8,128)S(1)} %get-tuple-element.23), channel_id=1, source_target_pairs={{0,5},{1,4},{2,9},{3,8},{4,23},{5,22},{6,27},{7,26},{8,7},{9,6},{1... | collective-permute-start | bytes 798728 | tf_op jit(solution)/shard_map/ppermute | solution.py:468
  59.3 0.8 dynamic_slice.9
  60.1 0.1 copy.10
  60.2 0.1 reshape.12
  60.3 0.1 reshape.13
  60.4 6.5 %collective-permute-done.7.refs_3_ = f32[520,128]{1,0:T(8,128)S(1)} collective-permute-done((f32[520,128]{1,0:T(8,128)}, f32[520,128]{1,0:T(8,128)S(1)}, u32[]{:S(2)}, u32[]{:S(2)}) %collective-permute-start.7) | collective-permute-done | bytes 266272 | tf_op jit(solution)/shard_map/ppermute | solution.py:468
  66.9 1.6 %collective-permute-done.8.refs_4_ = f32[520,128]{1,0:T(8,128)S(1)} collective-permute-done((f32[520,128]{1,0:T(8,128)}, f32[520,128]{1,0:T(8,128)S(1)}, u32[]{:S(2)}, u32[]{:S(2)}) %collective-permute-start.8) | collective-permute-done | bytes 266272 | tf_op jit(solution)/shard_map/ppermute | solution.py:468
  68.5 19.2 %collective-permute-done.9.refs_5_ = f32[520,128]{1,0:T(8,128)S(1)} collective-permute-done((f32[520,128]{1,0:T(8,128)}, f32[520,128]{1,0:T(8,128)S(1)}, u32[]{:S(2)}, u32[]{:S(2)}) %collective-permute-start.9) | collective-permute-done | bytes 266272 | tf_op jit(solution)/shard_map/ppermute | solution.py:468
  87.7 1.1 %collective-permute-done.11.refs_7_ = f32[520,128]{1,0:T(8,128)S(1)} collective-permute-done((f32[520,128]{1,0:T(8,128)S(1)}, f32[520,128]{1,0:T(8,128)S(1)}, u32[]{:S(2)}, u32[]{:S(2)}) %collective-permute-start.11) | collective-permute-done | bytes 266272 | tf_op jit(solution)/shard_map/ppermute | solution.py:468
  88.9 2.4 %gather_block.1 = (f32[32,128]{1,0:T(8,128)}, f32[32,128]{1,0:T(8,128)}, f32[32,32,512]{2,1,0:T(8,128)}) custom-call(f32[2,8,128]{2,1,0:T(8,128)S(1)} %pad.13.light_ref, f32[8,2,32,128]{3,2,1,0:T(8,128)S(1)} %all-to-all-done.parts_ref, f32[520,128]{1,0:T(8,128)S(1)} %collective-permute-done.4.refs_0_, f32[520,128]{1,0:T(8,128)S(1)} %collective-permute-done.5.refs_1_, ...), custom_call_target="tpu_custom_call" | custom-call | tf_op jit(solution)/shard_map/gather_block/pallas_call | solution.py:247
  (21 shorter events, 0.1 us)
Async XLA Ops:
  0.6 20.8 %copy-start = (s32[256,512]{1,0:T(8,128)S(1)}, s32[256,512]{1,0:T(8,128)}, u32[]{:S(2)}) copy-start(s32[256,512]{1,0:T(8,128)} %param.10) | copy-start | bytes 1572868
  0.6 15.3 %copy-start.2 = (f32[128,256]{1,0:T(8,128)S(1)}, f32[128,256]{1,0:T(8,128)}, u32[]{:S(2)}) copy-start(f32[128,256]{1,0:T(8,128)} %param.8) | copy-start | bytes 393220
  3.3 16.7 %collective-permute-start = (f32[2,256,128]{2,1,0:T(8,128)S(1)}, f32[2,256,128]{2,1,0:T(8,128)S(1)}, u32[]{:S(2)}, u32[]{:S(2)}) collective-permute-start(f32[2,256,128]{2,1,0:T(8,128)S(1)} %get-tuple-element.14), channel_id=1, source_target_pairs={{1,0},{2,1},{3,2},{4,3},{5,4},{6,5},{7,6},{9,8},{10,9},{11,10},{12... | collective-permute-start | bytes 786440 | tf_op jit(solution)/shard_map/ppermute | solution.py:443
  5.9 46.9 %collective-permute-start.4 = (f32[520,128]{1,0:T(8,128)S(1)}, f32[520,128]{1,0:T(8,128)S(1)}, u32[]{:S(2)}, u32[]{:S(2)}) collective-permute-start(f32[520,128]{1,0:T(8,128)S(1)} %get-tuple-element.17), channel_id=1, source_target_pairs={{0,0},{1,1},{2,12},{3,13},{4,18},{5,19},{6,30},{7,31},{8,2},{9,3},... | collective-permute-start | bytes 798728 | tf_op jit(solution)/shard_map/ppermute | solution.py:468
  9.0 45.4 %collective-permute-start.5 = (f32[520,128]{1,0:T(8,128)S(1)}, f32[520,128]{1,0:T(8,128)S(1)}, u32[]{:S(2)}, u32[]{:S(2)}) collective-permute-start(f32[520,128]{1,0:T(8,128)S(1)} %get-tuple-element.18), channel_id=1, source_target_pairs={{0,2},{1,3},{2,14},{3,15},{4,16},{5,17},{6,28},{7,29},{8,0},{9,1},... | collective-permute-start | bytes 798728 | tf_op jit(solution)/shard_map/ppermute | solution.py:468
  11.0 48.3 %collective-permute-start.6 = (f32[520,128]{1,0:T(8,128)S(1)}, f32[520,128]{1,0:T(8,128)S(1)}, u32[]{:S(2)}, u32[]{:S(2)}) collective-permute-start(f32[520,128]{1,0:T(8,128)S(1)} %get-tuple-element.19), channel_id=1, source_target_pairs={{0,4},{1,5},{2,8},{3,9},{4,22},{5,23},{6,26},{7,27},{8,6},{9,7},{1... | collective-permute-start | bytes 798728 | tf_op jit(solution)/shard_map/ppermute | solution.py:468
  16.0 18.9 %copy-start.1 = (f32[3,16]{1,0:T(4,128)S(1)}, f32[3,16]{1,0:T(4,128)}, u32[]{:S(2)}) copy-start(f32[3,16]{1,0:T(4,128)} %frac_ref.1) | copy-start | bytes 580
  20.2 5.9 %collective-permute-start.3 = (f32[3,64,128]{2,1,0:T(8,128)S(1)}, f32[3,64,128]{2,1,0:T(8,128)S(1)}, u32[]{:S(2)}, u32[]{:S(2)}) collective-permute-start(f32[3,64,128]{2,1,0:T(8,128)S(1)} %rim.1.small_ref), channel_id=1, source_target_pairs={{0,24},{8,16},{16,8},{24,0},{1,25},{9,17},{17,9},{25,1},{2,26},{10... | collective-permute-start | bytes 294920 | tf_op jit(solution)/shard_map/ppermute | solution.py:448
  21.4 12.2 %collective-permute-start.2 = (f32[3,64,128]{2,1,0:T(8,128)S(1)}, f32[3,64,128]{2,1,0:T(8,128)S(1)}, u32[]{:S(2)}, u32[]{:S(2)}) collective-permute-start(f32[3,64,128]{2,1,0:T(8,128)S(1)} %rim.1.small_ref), channel_id=1, source_target_pairs={{0,16},{8,24},{16,0},{24,8},{1,17},{9,25},{17,1},{25,9},{2,18},{10... | collective-permute-start | bytes 294920 | tf_op jit(solution)/shard_map/ppermute | solution.py:448
  26.1 7.6 %copy-start.3 = (f32[3,64,128]{2,1,0:T(8,128)}, f32[3,64,128]{2,1,0:T(8,128)S(1)}, u32[]{:S(2)}) copy-start(f32[3,64,128]{2,1,0:T(8,128)S(1)} %collective-permute-done.3.refs_2_) | copy-start | bytes 294916
  26.1 7.6 %collective-permute-start.1 = (f32[3,64,128]{2,1,0:T(8,128)S(1)}, f32[3,64,128]{2,1,0:T(8,128)S(1)}, u32[]{:S(2)}, u32[]{:S(2)}) collective-permute-start(f32[3,64,128]{2,1,0:T(8,128)S(1)} %rim.1.small_ref), channel_id=1, source_target_pairs={{0,8},{8,0},{16,24},{24,16},{1,9},{9,1},{17,25},{25,17},{2,10},{10... | collective-permute-start | bytes 294920 | tf_op jit(solution)/shard_map/ppermute | solution.py:448
  33.7 0.6 copy-start.4
  34.3 0.6 copy-start.5
  43.7 45.2 %all-to-all-start = ((f32[8,2,32,128]{3,2,1,0:T(8,128)}), f32[8,2,32,128]{3,2,1,0:T(8,128)S(1)}, u32[]{:S(2)}, u32[]{:S(2)}) async-start(f32[8,2,32,128]{3,2,1,0:T(8,128)} %march.1), calls=%async_computation | async-start | bytes 524288 | tf_op jit(solution)/shard_map/all_to_all | solution.py:484
  49.1 17.8 %collective-permute-start.7 = (f32[520,128]{1,0:T(8,128)}, f32[520,128]{1,0:T(8,128)S(1)}, u32[]{:S(2)}, u32[]{:S(2)}) collective-permute-start(f32[520,128]{1,0:T(8,128)} %get-tuple-element.20), channel_id=1, source_target_pairs={{0,6},{1,7},{2,10},{3,11},{4,20},{5,21},{6,24},{7,25},{8,4},{9,5},... | collective-permute-start | bytes 798728 | tf_op jit(solution)/shard_map/ppermute | solution.py:468
  52.2 16.3 %collective-permute-start.8 = (f32[520,128]{1,0:T(8,128)}, f32[520,128]{1,0:T(8,128)S(1)}, u32[]{:S(2)}, u32[]{:S(2)}) collective-permute-start(f32[520,128]{1,0:T(8,128)} %get-tuple-element.21), channel_id=1, source_target_pairs={{0,1},{1,0},{2,13},{3,12},{4,19},{5,18},{6,31},{7,30},{8,3},{9,2},... | collective-permute-start | bytes 798728 | tf_op jit(solution)/shard_map/ppermute | solution.py:468
  52.8 34.9 %collective-permute-start.9 = (f32[520,128]{1,0:T(8,128)}, f32[520,128]{1,0:T(8,128)S(1)}, u32[]{:S(2)}, u32[]{:S(2)}) collective-permute-start(f32[520,128]{1,0:T(8,128)} %get-tuple-element.22), channel_id=1, source_target_pairs={{0,3},{1,2},{2,15},{3,14},{4,17},{5,16},{6,29},{7,28},{8,1},{9,0},... | collective-permute-start | bytes 798728 | tf_op jit(solution)/shard_map/ppermute | solution.py:468
  54.3 33.4 %collective-permute-start.10 = (f32[520,128]{1,0:T(8,128)S(1)}, f32[520,128]{1,0:T(8,128)S(1)}, u32[]{:S(2)}, u32[]{:S(2)}) collective-permute-start(f32[520,128]{1,0:T(8,128)S(1)} %get-tuple-element.23), channel_id=1, source_target_pairs={{0,5},{1,4},{2,9},{3,8},{4,23},{5,22},{6,27},{7,26},{8,7},{9,6},{1... | collective-permute-start | bytes 798728 | tf_op jit(solution)/shard_map/ppermute | solution.py:468
  59.3 29.6 %collective-permute-start.11 = (f32[520,128]{1,0:T(8,128)S(1)}, f32[520,128]{1,0:T(8,128)S(1)}, u32[]{:S(2)}, u32[]{:S(2)}) collective-permute-start(f32[520,128]{1,0:T(8,128)S(1)} %get-tuple-element.24), channel_id=1, source_target_pairs={{0,7},{1,6},{2,11},{3,10},{4,21},{5,20},{6,25},{7,24},{8,5},{9,4},... | collective-permute-start | bytes 798728 | tf_op jit(solution)/shard_map/ppermute | solution.py:468
